TPU v7x, 32 devices: a 4x2x2 block of a 4x4x8 slice. The times are simulated.
32 devices in a mesh: dp: 4 (over y, z), ep: 8 (over x, core).
Axes of the slice: x: 4, y: 2, z: 2, core: 2. Of those that a mesh axis runs over, the one named last changes fastest.
The devices are a block of a 4x4x8 slice.
Arguments:
- x_tokens: bfloat16 [16384, 2048], P(('dp', 'ep')), parts along dimension 0
- dy_tokens: bfloat16 [16384, 2048], P(('dp', 'ep')), parts along dimension 0
- expert_ids: int32 [16384, 10], P(('dp', 'ep')), parts along dimension 0
- gate_vals: float32 [16384, 10], P(('dp', 'ep')), parts along dimension 0
- slot_pos: int32 [16384, 10], P(('dp', 'ep')), parts along dimension 0
- w_gate: bfloat16 [16, 2048, 512], P('ep')
- w_up: bfloat16 [16, 2048, 512], P('ep')
- w_down: bfloat16 [16, 512, 2048], P('ep')
- shared_gate: bfloat16 [2048, 512], replicated
- shared_up: bfloat16 [2048, 512], replicated
- shared_down: bfloat16 [512, 2048], replicated
Outputs:
- output 1: bfloat16 [16384, 2048], P(('dp', 'ep')), parts along dimension 0
- output 2: float32 [64, 2048, 512], P(('dp', 'ep')), parts along dimension 0
- output 3: float32 [64, 2048, 512], P(('dp', 'ep')), parts along dimension 0
- output 4: float32 [64, 512, 2048], P(('dp', 'ep')), parts along dimension 0
- output 5: float32 [32, 2048, 512], P(('dp', 'ep')), parts along dimension 0
- output 6: float32 [32, 2048, 512], P(('dp', 'ep')), parts along dimension 0
- output 7: float32 [32, 512, 2048], P(('dp', 'ep')), parts along dimension 0
There are 4 independent parts. A program takes and returns all parts, laid end to end along the dimension named above; an argument that names none is the same for every part.
All inputs are finite; a program needn't handle non-finite values.
Results may differ from a plain program's by a relative error of at most 0.00172.
Values are sent between devices in bfloat16 or wider.
A program may use at most 768 MiB of HBM per device.

v0:
```python
import jax
import jax.numpy as jnp
from jax import lax
from jax.sharding import PartitionSpec as P


def swiglu_parts(act_gate, act_up, grad_hidden):
    gate_f32 = act_gate.astype(jnp.float32)
    up_f32 = act_up.astype(jnp.float32)
    sigma = jax.nn.sigmoid(gate_f32)
    silu_gate = gate_f32 * sigma
    hidden = (silu_gate * up_f32).astype(jnp.bfloat16)
    grad_gate = (grad_hidden * up_f32 * sigma * (1.0 + gate_f32 * (1.0 - sigma))).astype(jnp.bfloat16)
    grad_up = (grad_hidden * silu_gate).astype(jnp.bfloat16)
    return hidden, grad_gate, grad_up


def slot_tables(expert_ids, slot_pos, gate_vals, num_experts, capacity):
    tok_count, top_k = expert_ids.shape
    slot_total = num_experts * capacity
    copy_slot = jnp.where(slot_pos >= 0, expert_ids * capacity + slot_pos, slot_total).reshape(-1)
    copy_token = jnp.broadcast_to(jnp.arange(tok_count, dtype=jnp.int32)[:, None], (tok_count, top_k)).reshape(-1)
    slot_token = jnp.full((slot_total + 1,), tok_count, jnp.int32).at[copy_slot].set(copy_token)[:slot_total]
    slot_gate = jnp.zeros((slot_total + 1,), jnp.float32).at[copy_slot].set(gate_vals.reshape(-1))[:slot_total]
    return copy_slot, slot_token, slot_gate


def take_rows(rows, row_index):
    return jnp.take(rows, row_index, axis=0, mode='fill', fill_value=0)


def shared_backward(x_tokens, dy_tokens, shared_gate, shared_up, shared_down):
    act_gate = jnp.dot(x_tokens, shared_gate, preferred_element_type=jnp.float32).astype(jnp.bfloat16)
    act_up = jnp.dot(x_tokens, shared_up, preferred_element_type=jnp.float32).astype(jnp.bfloat16)
    grad_hidden = jnp.einsum('td,fd->tf', dy_tokens, shared_down, preferred_element_type=jnp.float32)
    hidden, grad_gate, grad_up = swiglu_parts(act_gate, act_up, grad_hidden)
    grad_gate_w = jnp.einsum('td,tf->df', x_tokens, grad_gate, preferred_element_type=jnp.float32)
    grad_up_w = jnp.einsum('td,tf->df', x_tokens, grad_up, preferred_element_type=jnp.float32)
    grad_down_w = jnp.einsum('tf,td->fd', hidden, dy_tokens, preferred_element_type=jnp.float32)
    grad_input = jnp.einsum('tf,df->td', grad_gate, shared_gate, preferred_element_type=jnp.float32) + jnp.einsum('tf,df->td', grad_up, shared_up, preferred_element_type=jnp.float32)
    return grad_input, grad_gate_w, grad_up_w, grad_down_w


def solution(mesh):
    group = mesh.shape['ep']
    token_spec = P(('dp', 'ep'), None)
    expert_spec = P('ep', None, None)
    whole_spec = P(None, None)
    grad_spec = P(('dp', 'ep'), None, None)

    def local_backward(x_tokens, dy_tokens, expert_ids, gate_vals, slot_pos, w_gate, w_up, w_down, shared_gate, shared_up, shared_down):
        tok_count, top_k = expert_ids.shape
        local_experts, model_dim, expert_ff = w_gate.shape
        num_experts = local_experts * group
        capacity = (3 * tok_count * top_k + 2 * num_experts - 1) // (2 * num_experts)
        copy_slot, slot_token, slot_gate = slot_tables(expert_ids, slot_pos, gate_vals, num_experts, capacity)
        send_x = take_rows(x_tokens, slot_token).reshape(num_experts, capacity, model_dim)
        dy_rows = take_rows(dy_tokens, slot_token)
        send_dz = (dy_rows.astype(jnp.float32) * slot_gate[:, None]).astype(jnp.bfloat16).reshape(num_experts, capacity, model_dim)
        x_exp = lax.all_to_all(send_x, 'ep', 0, 1, tiled=True)
        dz_exp = lax.all_to_all(send_dz, 'ep', 0, 1, tiled=True)
        act_gate = jnp.einsum('erd,edf->erf', x_exp, w_gate, preferred_element_type=jnp.float32).astype(jnp.bfloat16)
        act_up = jnp.einsum('erd,edf->erf', x_exp, w_up, preferred_element_type=jnp.float32).astype(jnp.bfloat16)
        grad_hidden = jnp.einsum('erd,efd->erf', dz_exp, w_down, preferred_element_type=jnp.float32)
        hidden, grad_gate, grad_up = swiglu_parts(act_gate, act_up, grad_hidden)
        grad_w_gate = jnp.einsum('erd,erf->edf', x_exp, grad_gate, preferred_element_type=jnp.float32)
        grad_w_up = jnp.einsum('erd,erf->edf', x_exp, grad_up, preferred_element_type=jnp.float32)
        grad_w_down = jnp.einsum('erf,erd->efd', hidden, dz_exp, preferred_element_type=jnp.float32)
        grad_exp = (jnp.einsum('erf,edf->erd', grad_gate, w_gate, preferred_element_type=jnp.float32) + jnp.einsum('erf,edf->erd', grad_up, w_up, preferred_element_type=jnp.float32)).astype(jnp.bfloat16)
        returned = lax.all_to_all(grad_exp, 'ep', 1, 0, tiled=True).reshape(num_experts * capacity, model_dim)
        copies = take_rows(returned, copy_slot).reshape(tok_count, top_k, model_dim)
        routed_sum = jnp.sum(copies.astype(jnp.float32), axis=1)
        shared_dx, grad_shared_gate, grad_shared_up, grad_shared_down = shared_backward(x_tokens, dy_tokens, shared_gate, shared_up, shared_down)
        grad_x = (routed_sum + shared_dx).astype(jnp.bfloat16)
        return grad_x, grad_w_gate, grad_w_up, grad_w_down, grad_shared_gate[None], grad_shared_up[None], grad_shared_down[None]

    return jax.shard_map(local_backward, mesh=mesh, in_specs=(token_spec, token_spec, token_spec, token_spec, token_spec, expert_spec, expert_spec, expert_spec, whole_spec, whole_spec, whole_spec), out_specs=(token_spec, grad_spec, grad_spec, grad_spec, grad_spec, grad_spec, grad_spec), check_vma=False)
```

profile of v0, /device:TPU:81, one launch (start us, length us, event | category | flops | bytes accessed | tf_op | source)
XLA Modules:
  0.0 1505.0 jit_solution(5583547667914043644)
XLA Ops:
  0.6 0.0 copy-start
  0.6 1.5 compare_and_fusion.1
  2.2 0.1 copy.37
  2.3 0.2 reshape.101
  2.5 0.6 compare_select_fusion
  3.2 0.2 reshape.135
  3.4 0.4 copy-done.11
  3.8 19.3 %scatter_custom_fusion = s32[7681]{0:T(1024)S(1)} fusion(s32[5120]{0:T(1024)S(1)} %bitcast.68, s32[5120]{0:T(1024)S(1)} %reshape.135, s32[]{:T(128)} %constant.14.clone.1), kind=kCustom, calls=%fused_computation.56 | custom fusion | bytes 30728 | tf_op jit(solution)/shard_map/scatter | solution.py:23
  23.1 0.0 copy-done
  23.1 29.5 %gather_fusion.2 = bf16[7680,2048]{1,0:T(8,128)(2,1)} fusion(bf16[512,2048]{1,0:T(8,128)(2,1)S(1)} %copy-done, s32[8192]{0:T(1024)S(1)} %pad_clamp_fusion), kind=kCustom, calls=%fused_computation.1.clone | custom fusion | bytes 62945280 | tf_op jit(solution)/shard_map/jit(_take)/gather | solution.py:29
  52.7 21.5 %broadcast_select_fusion = bf16[7680,2048]{1,0:T(8,128)(2,1)} fusion(bf16[7680,2048]{1,0:T(8,128)(2,1)} %gather_fusion.2, pred[7680]{0:T(1024)(128)(4,1)S(1)} %compare_and_fusion), kind=kLoop, calls=%fused_computation.8 | loop fusion | flops 15728640 | bytes 62922240 | tf_op jit(solution)/shard_map/jit(_take)/select_n | solution.py:29
  74.1 9.0 all-to-all-start.1
  83.1 0.0 copy-done.9
  83.1 0.1 copy.38
  83.3 0.2 reshape.143
  83.5 59.4 %gather_fusion.1 = bf16[7680,2048]{1,0:T(8,128)(2,1)} fusion(bf16[512,2048]{1,0:T(8,128)(2,1)} %param.14, s32[8192]{0:T(1024)S(1)} %pad_clamp_fusion), kind=kCustom, calls=%fused_computation.clone | custom fusion | bytes 62945280 | tf_op jit(solution)/shard_map/jit(_take)/gather | solution.py:29
  142.8 19.4 %scatter_custom_fusion.1 = f32[7681]{0:T(1024)S(1)} fusion(s32[5120]{0:T(1024)} %bitcast.69, f32[5120]{0:T(1024)S(1)} %reshape.143, f32[]{:T(128)} %constant.23.clone.1), kind=kCustom, calls=%fused_computation.54 | custom fusion | bytes 31236 | tf_op jit(solution)/shard_map/scatter | solution.py:24
  162.3 21.8 %multiply_convert_fusion = bf16[7680,2048]{1,0:T(8,128)(2,1)} fusion(bf16[7680,2048]{1,0:T(8,128)(2,1)} %gather_fusion.1, f32[7680]{0:T(1024)S(1)} %bitcast.66, pred[7680]{0:T(1024)(128)(4,1)S(1)} %compare_and_fusion), kind=kLoop, calls=%fused_computation.7 | loop fusion | flops 62914560 | bytes 62952960 | tf_op jit(solution)/shard_map/convert_element_type | solution.py:59
  184.1 239.8 %all-to-all-done.1 = bf16[16,480,2048]{2,1,0:T(8,128)(2,1)} async-done(((bf16[16,480,2048]{2,1,0:T(8,128)(2,1)}), bf16[16,480,2048]{2,1,0:T(8,128)(2,1)}, u32[]{:S(2)}, u32[]{:S(2)}) %all-to-all-start.1) | async-done | bytes 31457312 | tf_op jit(solution)/shard_map/all_to_all | solution.py:60
  423.9 8.2 all-to-all-start
  432.2 21.4 %copy.40 = bf16[2,8,480,2048]{3,2,1,0:T(8,128)(2,1)} copy(bf16[2,8,480,2048]{3,2,0,1:T(8,128)(2,1)} %bitcast.7) | data formatting | bytes 62914560 | tf_op jit(solution)/shard_map/all_to_all | solution.py:60
  453.6 23.6 %convolution_convert_fusion = bf16[2,3840,512]{2,1,0:T(8,128)(2,1)} fusion(bf16[2,3840,2048]{2,1,0:T(8,128)(2,1)} %bitcast.60, bf16[2,2048,512]{2,1,0:T(8,128)(2,1)} %param.18), kind=kOutput, calls=%fused_computation.24 | convolution fusion | flops 16110059520 | bytes 43515904 | tf_op jit(solution)/shard_map/erd,edf->erf/dot_general | solution.py:62
  477.2 0.0 copy-done.12
  477.2 22.4 %convolution_convert_fusion.1 = bf16[2,3840,512]{2,1,0:T(8,128)(2,1)} fusion(bf16[2,3840,2048]{2,1,0:T(8,128)(2,1)} %bitcast.61, bf16[2,2048,512]{2,1,0:T(8,128)(2,1)S(1)} %copy-done.12), kind=kOutput, calls=%fused_computation.25 | convolution fusion | flops 16110059520 | bytes 43515904 | tf_op jit(solution)/shard_map/erd,edf->erf/dot_general | solution.py:63
  499.6 273.2 %all-to-all-done = bf16[16,480,2048]{2,1,0:T(8,128)(2,1)} async-done(((bf16[16,480,2048]{2,1,0:T(8,128)(2,1)}), bf16[16,480,2048]{2,1,0:T(8,128)(2,1)}, u32[]{:S(2)}, u32[]{:S(2)}) %all-to-all-start) | async-done | bytes 31457312 | tf_op jit(solution)/shard_map/all_to_all | solution.py:61
  772.8 21.4 %copy.39 = bf16[2,8,480,2048]{3,2,1,0:T(8,128)(2,1)} copy(bf16[2,8,480,2048]{3,2,0,1:T(8,128)(2,1)} %bitcast.3) | data formatting | bytes 62914560 | tf_op jit(solution)/shard_map/all_to_all | solution.py:61
  794.2 32.7 %multiply_convert_fusion.1 = (bf16[2,3840,512]{2,1,0:T(8,128)(2,1)}, bf16[2,3840,512]{2,1,0:T(8,128)(2,1)}) fusion(bf16[2,3840,512]{2,1,0:T(8,128)(2,1)} %convolution_convert_fusion, bf16[2,3840,512]{2,1,0:T(8,128)(2,1)} %convolution_convert_fusion.1, bf16[2,3840,2048]{2,1,0:T(8,128)(2,1)} %bitcast.64, bf16[2,512,2048]{2,1,0:T(8,128)(2,1)} %param.20), kind=kOutput, calls=%fused_computation.22 | convolution fusion | flops 16165109760 | bytes 67108864 | tf_op jit(solution)/shard_map/erd,efd->erf/dot_general | solution.py:64
  827.0 29.7 %fusion.25 = f32[2,3840,2048]{2,1,0:T(8,128)} fusion(bf16[2,3840,512]{2,1,0:T(8,128)(2,1)} %get-tuple-element.32, bf16[2,2048,512]{2,1,0:T(8,128)(2,1)} %param.18), kind=kOutput, calls=%fused_computation.61 | convolution fusion | flops 16106127360 | bytes 74973184 | tf_op jit(solution)/shard_map/erf,edf->erd/dot_general | solution.py:69
  856.7 36.6 %add_convert_fusion = bf16[2,3840,2048]{2,1,0:T(8,128)(2,1)} fusion(f32[2,3840,2048]{2,1,0:T(8,128)} %fusion.25, bf16[2,3840,512]{2,1,0:T(8,128)(2,1)} %get-tuple-element.31, bf16[2,2048,512]{2,1,0:T(8,128)(2,1)} %param.19), kind=kOutput, calls=%fused_computation.6 | convolution fusion | flops 16137584640 | bytes 106430464 | tf_op jit(solution)/shard_map/erf,edf->erd/dot_general | solution.py:69
  893.3 56.5 %copy.41 = bf16[2,3840,2048]{2,0,1:T(2,128)(2,1)} copy(bf16[2,3840,2048]{2,1,0:T(8,128)(2,1)} %add_convert_fusion) | data formatting | bytes 62914560 | tf_op jit(solution)/shard_map/convert_element_type | solution.py:69
  949.7 8.0 all-to-all-start.2
  957.7 0.0 copy-done.10
  957.8 0.8 copy.36
  958.5 3.0 convolution_convert_fusion.2
  961.5 0.0 copy-start.4
  961.5 3.0 convolution_convert_fusion.3
  964.6 0.0 copy-done.1
  964.6 0.0 copy-done.13
  964.6 0.0 copy-start.14
  964.6 2.4 fusion.12
  967.0 0.0 copy-done.14
  967.0 3.3 convolution_bitcast_fusion.2
  970.3 5.3 copy.46
  975.7 4.6 convolution_bitcast_fusion.1
  980.2 5.3 copy.47
  985.6 0.0 copy-done.8
  985.6 0.6 broadcast_clamp_fusion
  986.2 5.0 fusion.26
  991.2 0.0 copy-done.4
  991.2 0.0 copy-done.2
  991.2 0.0 copy-done.15
  991.2 0.0 slice-start.1
  991.2 3.4 convolution_bitcast_fusion
  994.7 0.0 slice-done
  994.7 22.0 %fusion.28 = f32[2,2048,512]{2,1,0:T(8,128)} fusion(bf16[2,3840,2048]{2,1,0:T(8,128)(2,1)} %bitcast.62, bf16[2,3840,512]{2,1,0:T(8,128)(2,1)S(1)} %bitcast.71), kind=kOutput, calls=%fused_computation.64 | convolution fusion | flops 16106127360 | bytes 47710208 | tf_op jit(solution)/shard_map/erd,erf->edf/dot_general | solution.py:67
  1016.7 23.9 %fusion.27 = f32[2,2048,512]{2,1,0:T(8,128)} fusion(bf16[2,3840,2048]{2,1,0:T(8,128)(2,1)} %bitcast.63, bf16[2,3840,512]{2,1,0:T(8,128)(2,1)} %get-tuple-element.32), kind=kOutput, calls=%fused_computation.63 | convolution fusion | flops 16106127360 | bytes 47710208 | tf_op jit(solution)/shard_map/erd,erf->edf/dot_general | solution.py:66
  1040.6 28.0 %fusion.8 = f32[2,512,2048]{2,1,0:T(8,128)} fusion(bf16[2,3840,2048]{2,1,0:T(8,128)(2,1)} %bitcast.65, bf16[2,3840,512]{2,1,0:T(8,128)(2,1)} %convolution_convert_fusion.1, bf16[2,3840,512]{2,1,0:T(8,128)(2,1)} %convolution_convert_fusion), kind=kOutput, calls=%fused_computation.23 | convolution fusion | flops 16137584640 | bytes 55574528 | tf_op jit(solution)/shard_map/erf,erd->efd/dot_general | solution.py:68
  1068.5 230.0 %all-to-all-done.2 = bf16[2,3840,2048]{2,0,1:T(2,128)(2,1)} async-done(((bf16[2,3840,2048]{2,0,1:T(2,128)(2,1)}), bf16[2,3840,2048]{2,0,1:T(2,128)(2,1)}, u32[]{:S(2)}, u32[]{:S(2)}) %all-to-all-start.2) | async-done | bytes 31457312 | tf_op jit(solution)/shard_map/all_to_all | solution.py:70
  1298.5 21.9 %copy.42 = bf16[2,8,480,2048]{3,2,0,1:T(8,128)(2,1)} copy(bf16[2,8,480,2048]{3,0,2,1:T(2,128)(2,1)} %bitcast.9) | data formatting | bytes 62914560 | tf_op jit(solution)/shard_map/all_to_all | solution.py:70
  1320.5 0.0 copy-done.7
  1320.5 119.6 %gather_fusion = bf16[5120,2048]{1,0:T(8,128)(2,1)} fusion(bf16[7680,2048]{1,0:T(8,128)(2,1)} %bitcast.57, s32[5120]{0:T(1024)S(1)} %copy-done.7), kind=kCustom, calls=%fused_computation.2 | custom fusion | bytes 41963520 | tf_op jit(solution)/shard_map/jit(_take)/gather | solution.py:29
  1440.1 34.1 %gather.10 = bf16[512,10,2048]{2,1,0:T(8,128)(2,1)} reshape(bf16[5120,2048]{1,0:T(8,128)(2,1)} %gather_fusion) | data formatting | bytes 41943040 | tf_op jit(solution)/shard_map/jit(_take)/gather | solution.py:29
  1474.2 24.0 %convert_reduce_fusion = f32[512,2048]{1,0:T(8,128)} fusion(bf16[512,10,2048]{2,1,0:T(8,128)(2,1)} %gather.10, pred[512,10]{1,0:T(8,128)(4,1)S(1)} %copy-done.6), kind=kLoop, calls=%fused_computation.5 | loop fusion | flops 30408704 | bytes 25170944 | tf_op jit(solution)/shard_map/reduce_sum | solution.py:72
  1498.1 6.5 add_convert_fusion.1
  (23 shorter events, 0.1 us)
Async XLA Ops:
  0.6 22.5 %copy-start = (bf16[512,2048]{1,0:T(8,128)(2,1)S(1)}, bf16[512,2048]{1,0:T(8,128)(2,1)}, u32[]{:S(2)}) copy-start(bf16[512,2048]{1,0:T(8,128)(2,1)} %param.13) | copy-start | bytes 6291460
  3.2 0.6 copy-start.11
  74.1 9.0 copy-start.9
  74.1 349.8 %all-to-all-start.1 = ((bf16[16,480,2048]{2,1,0:T(8,128)(2,1)}), bf16[16,480,2048]{2,1,0:T(8,128)(2,1)}, u32[]{:S(2)}, u32[]{:S(2)}) async-start(bf16[16,480,2048]{2,1,0:T(8,128)(2,1)} %bitcast.58), calls=%async_computation.1 | async-start | bytes 62914560 | tf_op jit(solution)/shard_map/all_to_all | solution.py:60
  423.9 348.9 %all-to-all-start = ((bf16[16,480,2048]{2,1,0:T(8,128)(2,1)}), bf16[16,480,2048]{2,1,0:T(8,128)(2,1)}, u32[]{:S(2)}, u32[]{:S(2)}) async-start(bf16[16,480,2048]{2,1,0:T(8,128)(2,1)} %bitcast.59), calls=%async_computation | async-start | bytes 62914560 | tf_op jit(solution)/shard_map/all_to_all | solution.py:61
  453.6 23.6 %copy-start.12 = (bf16[2,2048,512]{2,1,0:T(8,128)(2,1)S(1)}, bf16[2,2048,512]{2,1,0:T(8,128)(2,1)}, u32[]{:S(2)}) copy-start(bf16[2,2048,512]{2,1,0:T(8,128)(2,1)} %param.19) | copy-start | bytes 12582916
  949.7 8.0 copy-start.10
  949.7 348.8 %all-to-all-start.2 = ((bf16[2,3840,2048]{2,0,1:T(2,128)(2,1)}), bf16[2,3840,2048]{2,0,1:T(2,128)(2,1)}, u32[]{:S(2)}, u32[]{:S(2)}) async-start(bf16[2,3840,2048]{2,0,1:T(2,128)(2,1)} %copy.41), calls=%async_computation.2 | async-start | bytes 62914560 | tf_op jit(solution)/shard_map/all_to_all | solution.py:70
  958.5 6.0 copy-start.1
  958.5 6.1 copy-start.13
  961.5 29.7 %copy-start.4 = (bf16[512,512]{1,0:T(8,128)(2,1)}, bf16[512,512]{1,0:T(8,128)(2,1)S(1)}, u32[]{:S(2)}) copy-start(bf16[512,512]{1,0:T(8,128)(2,1)S(1)} %convolution_convert_fusion.2) | copy-start | bytes 1572868
  964.6 2.4 copy-start.14
  975.7 9.9 copy-start.8
  985.6 5.6 copy-start.2
  985.6 5.6 copy-start.15
  986.2 8.5 slice-start
  991.2 3.4 slice-start.1
  1298.5 21.9 %copy-start.7 = (s32[5120]{0:T(1024)S(1)}, s32[5120]{0:T(1024)}, u32[]{:S(2)}) copy-start(s32[5120]{0:T(1024)} %broadcast_clamp_fusion) | copy-start | bytes 61444
  1440.1 34.1 %copy-start.6 = (pred[512,10]{1,0:T(8,128)(4,1)S(1)}, pred[512,10]{1,0:T(8,128)(4,1)}, u32[]{:S(2)}) copy-start(pred[512,10]{1,0:T(8,128)(4,1)} %copy.36) | copy-start | bytes 15364
  1474.2 24.0 %copy-start.3 = (bf16[2048,512]{1,0:T(8,128)(2,1)S(1)}, bf16[2048,512]{1,0:T(8,128)(2,1)}, u32[]{:S(2)}) copy-start(bf16[2048,512]{1,0:T(8,128)(2,1)} %param.22) | copy-start | bytes 6291460
  1474.2 24.0 %copy-start.5 = (bf16[512,512]{1,0:T(8,128)(2,1)S(1)}, bf16[512,512]{1,0:T(8,128)(2,1)}, u32[]{:S(2)}) copy-start(bf16[512,512]{1,0:T(8,128)(2,1)} %copy-done.4) | copy-start | bytes 1572868
where the time goes:
time: 1520 us; the launch traced here: 1510 us
  waiting for transfers between devices  743 us (49%)
  local copies, waits for them, and re-layouts  415 us (27%)
  matrix products  250 us (16%)
  other arithmetic  70.1 us (5%)
  starting transfers between devices  25.2 us (2%)
    all_to_all x1, waiting for transfers between devices, local_backward(): dz_exp = lax.all_to_all(send_dz, 'ep', 0, 1, tiled=True)  273 us
    gather x4, local copies, waits for them, and re-layouts, take_rows(): return jnp.take(rows, row_index, axis=0, mode='fill', fill_value=0)  243 us
    all_to_all x1, waiting for transfers between devices, local_backward(): x_exp = lax.all_to_all(send_x, 'ep', 0, 1, tiled=True)  240 us
    all_to_all x1, waiting for transfers between devices, local_backward(): lax.all_to_all(grad_exp, 'ep', 1, 0, tiled=True)  230 us
    convert_element_type x1, local copies, waits for them, and re-layouts, local_backward(): (jnp.einsum('erf,edf->erd', grad_gate, w_gate, preferred_element_type=jnp...  56.5 us
    dot_general x1, matrix products, local_backward(): jnp.einsum('erf,edf->erd', grad_up, w_up, preferred_element_type=jnp.floa...  36.6 us
    dot_general x1, matrix products, local_backward(): jnp.einsum('erd,efd->erf', dz_exp, w_down, preferred_element_type=jnp.flo...  32.7 us
  transfers between devices with their start and end apart: 3, of which 3 were waited for; matrix products, arithmetic and copies ran while one was open for 19% of the time, Pallas kernels for 0%

commit v1 on v0

v1 whole, which is shorter than its diff:
```python
import jax
import jax.numpy as jnp
from jax import lax
from jax.sharding import PartitionSpec as P

S = 2


def swiglu_parts(act_gate, act_up, grad_hidden):
    gate_f32 = act_gate.astype(jnp.float32)
    up_f32 = act_up.astype(jnp.float32)
    sigma = jax.nn.sigmoid(gate_f32)
    silu_gate = gate_f32 * sigma
    hidden = (silu_gate * up_f32).astype(jnp.bfloat16)
    grad_gate = (grad_hidden * up_f32 * sigma * (1.0 + gate_f32 * (1.0 - sigma))).astype(jnp.bfloat16)
    grad_up = (grad_hidden * silu_gate).astype(jnp.bfloat16)
    return hidden, grad_gate, grad_up


def dot(spec, a, b):
    return jnp.einsum(spec, a, b, preferred_element_type=jnp.float32)


def shared_backward(x_tokens, dy_tokens, shared_gate, shared_up, shared_down):
    act_gate = dot('td,df->tf', x_tokens, shared_gate).astype(jnp.bfloat16)
    act_up = dot('td,df->tf', x_tokens, shared_up).astype(jnp.bfloat16)
    grad_hidden = dot('td,fd->tf', dy_tokens, shared_down)
    hidden, grad_gate, grad_up = swiglu_parts(act_gate, act_up, grad_hidden)
    grad_gate_w = dot('td,tf->df', x_tokens, grad_gate)
    grad_up_w = dot('td,tf->df', x_tokens, grad_up)
    grad_down_w = dot('tf,td->fd', hidden, dy_tokens)
    grad_input = dot('tf,df->td', grad_gate, shared_gate) + dot('tf,df->td', grad_up, shared_up)
    return grad_input, grad_gate_w, grad_up_w, grad_down_w


def solution(mesh):
    group = mesh.shape['ep']
    token_spec = P(('dp', 'ep'), None)
    expert_spec = P('ep', None, None)
    whole_spec = P(None, None)
    grad_spec = P(('dp', 'ep'), None, None)

    def local_backward(x_tokens, dy_tokens, expert_ids, gate_vals, slot_pos, w_gate, w_up, w_down, shared_gate, shared_up, shared_down):
        tok_count, top_k = expert_ids.shape
        local_experts, model_dim, expert_ff = w_gate.shape
        num_experts = local_experts * group
        step = tok_count // S
        table = jnp.full((tok_count, num_experts), jnp.inf, jnp.float32)
        experts = jnp.arange(num_experts, dtype=jnp.int32)[None, :]
        for j in range(top_k):
            hit = (expert_ids[:, j:j + 1] == experts) & (slot_pos[:, j:j + 1] >= 0)
            table = jnp.where(hit, gate_vals[:, j:j + 1], table)
        table_all = lax.all_gather(table, 'ep')
        mine = lax.dynamic_slice_in_dim(table_all, lax.axis_index('ep') * local_experts, local_experts, axis=2)
        routed = []
        parts = []
        for s in range(S):
            rows = slice(s * step, (s + 1) * step)
            x_all = lax.all_gather(x_tokens[rows], 'ep', tiled=True)
            dy_all = lax.all_gather(dy_tokens[rows], 'ep', tiled=True)
            total = 0.0
            for e in range(local_experts):
                gate = mine[:, rows, e].reshape(-1, 1)
                kept = gate < jnp.inf
                z = (dy_all.astype(jnp.float32) * jnp.where(kept, gate, 0.0)).astype(jnp.bfloat16)
                act_gate = jnp.where(kept, dot('td,df->tf', x_all, w_gate[e]), 0.0).astype(jnp.bfloat16)
                act_up = jnp.where(kept, dot('td,df->tf', x_all, w_up[e]), 0.0).astype(jnp.bfloat16)
                grad_hidden = dot('td,fd->tf', z, w_down[e])
                hidden, grad_gate, grad_up = swiglu_parts(act_gate, act_up, grad_hidden)
                parts.append((e, x_all, z, hidden, grad_gate, grad_up))
                r = dot('tf,df->td', grad_gate, w_gate[e]) + dot('tf,df->td', grad_up, w_up[e])
                total = total + lax.reduce_precision(r, 8, 7)
            routed.append(lax.psum_scatter(total, 'ep', scatter_dimension=0, tiled=True))
        dgs, dus, dds = [], [], []
        for e in range(local_experts):
            dg = du = dd = 0.0
            for (pe, x_all, z, hidden, grad_gate, grad_up) in parts:
                if pe == e:
                    dg = dg + dot('td,tf->df', x_all, grad_gate)
                    du = du + dot('td,tf->df', x_all, grad_up)
                    dd = dd + dot('tf,td->fd', hidden, z)
            dgs.append(dg)
            dus.append(du)
            dds.append(dd)
        routed_sum = jnp.concatenate(routed, axis=0)
        shared_dx, grad_shared_gate, grad_shared_up, grad_shared_down = shared_backward(x_tokens, dy_tokens, shared_gate, shared_up, shared_down)
        grad_x = (routed_sum + shared_dx).astype(jnp.bfloat16)
        return grad_x, jnp.stack(dgs), jnp.stack(dus), jnp.stack(dds), grad_shared_gate[None], grad_shared_up[None], grad_shared_down[None]

    return jax.shard_map(local_backward, mesh=mesh, in_specs=(token_spec, token_spec, token_spec, token_spec, token_spec, expert_spec, expert_spec, expert_spec, whole_spec, whole_spec, whole_spec), out_specs=(token_spec, grad_spec, grad_spec, grad_spec, grad_spec, grad_spec, grad_spec), check_vma=False)
```

time: 1520 us -> 483 us (0.32)
  waiting for transfers between devices: 743 us -> 65.9 us
  local copies, waits for them, and re-layouts: 415 us -> 42 us
  matrix products: 250 us -> 326 us
  other arithmetic: 70.1 us -> 12.6 us
  starting transfers between devices: 25.2 us -> 0.38 us
    all_to_all x3 -> x0, waiting for transfers between devices: 743 us -> none  [the longest x1 273 us: local_backward(): dz_exp = lax.all_to_all(send_dz, 'ep', 0, 1, tiled=True)]
    gather x4 -> x0, local copies, waits for them, and re-layouts: 243 us -> none  [take_rows(): return jnp.take(rows, row_index, axis=0, mode='fill', fill_value=0)]
    dot_general x16 -> x40, matrix products: 250 us -> 326 us  [dot(): return jnp.einsum(spec, a, b, preferred_element_type=jnp.float32)]
    all_to_all x3 -> x0, local copies, waits for them, and re-layouts: 64.7 us -> none  [the longest x1 21.9 us: local_backward(): lax.all_to_all(grad_exp, 'ep', 1, 0, tiled=True)]
    all_gather x0 -> x4, waiting for transfers between devices: none -> 64.4 us  [the longest x2 33.2 us: local_backward(): dy_all = lax.all_gather(dy_tokens[rows], 'ep', tiled=True)]
    convert_element_type x1 -> x0, local copies, waits for them, and re-layouts: 56.5 us -> none  [local_backward(): (jnp.einsum('erf,edf->erd', grad_gate, w_gate, preferred_element_type=jnp...]
    scatter x2 -> x0, local copies, waits for them, and re-layouts: 38.7 us -> none  [the longest x1 19.4 us: slot_tables(): jnp.zeros((slot_total + 1,), jnp.float32).at[copy_slot]]
    all_to_all x3 -> x0, starting transfers between devices: 25.2 us -> none  [the longest x1 9 us: local_backward(): x_exp = lax.all_to_all(send_x, 'ep', 0, 1, tiled=True)]
  transfers between devices with their start and end apart: 3 -> 6, of which waited for: 3 -> 2; matrix products, arithmetic and copies ran while one was open for 19% -> 76% of each run, Pallas kernels for 0% -> 0%
where the time goes in v1:
time: 483 us; the launch traced here: 478 us
  matrix products  326 us (67%)
  waiting for transfers between devices  65.9 us (14%)
  local copies, waits for them, and re-layouts  42 us (9%)
  between operations  15.4 us (3%)
  blocking collectives  15.2 us (3%)
  other arithmetic  12.6 us (3%)
    dot_general x40, matrix products, dot(): return jnp.einsum(spec, a, b, preferred_element_type=jnp.float32)  326 us
    unnamed x148, local copies, waits for them, and re-layouts  35.5 us
    all_gather x2, waiting for transfers between devices, local_backward(): dy_all = lax.all_gather(dy_tokens[rows], 'ep', tiled=True)  33.2 us
    all_gather x2, waiting for transfers between devices, local_backward(): x_all = lax.all_gather(x_tokens[rows], 'ep', tiled=True)  31.3 us
    all_gather x1, blocking collectives, local_backward(): table_all = lax.all_gather(table, 'ep')  15.2 us
  transfers between devices with their start and end apart: 6, of which 2 were waited for; matrix products, arithmetic and copies ran while one was open for 76% of the time, Pallas kernels for 0%

profile of v1, /device:TPU:81, one launch (start us, length us, event | category | flops | bytes accessed | tf_op | source)
XLA Modules:
  0.0 477.6 jit_solution(13566018046513075756)
XLA Ops:
  7.3 3.2 fusion.133
  10.6 3.1 fusion.134
  13.9 0.7 all-gather.11.cloned.1.call-update
  14.7 0.6 all-gather.9.cloned.1.call-update
  15.4 0.1 compare_reduce_fusion.9
  15.5 0.1 select_select_fusion
  15.6 15.2 %all_gather.17 = f32[8,512,16]{1,2,0:T(8,128)S(1)} all-gather(f32[1,512,16]{1,2,0:T(8,128)S(1)} %select_select_fusion), channel_id=1, replica_groups=mesh['dp'=4,'ep'=8] {'ep'}, dimensions={0}, use_global_device_ids=true | all-gather | bytes 294912 | tf_op jit(solution)/shard_map/all_gather | solution.py:53
  30.8 0.1 constant_dynamic-slice_fusion.2
  31.0 31.2 %all-gather.7.cloned.1.call-done = bf16[2048,2048]{1,0:T(8,128)(2,1)} async-done(((bf16[256,2048]{1,0:T(8,128)(2,1)}), bf16[2048,2048]{1,0:T(8,128)(2,1)}) %all-gather.7.cloned.1.call-update) | async-done | bytes 8388624 | tf_op jit(solution)/shard_map/all_gather | solution.py:59
  62.2 10.0 %select_convert_fusion.4 = bf16[2048,512]{1,0:T(8,128)(2,1)} fusion(bf16[2048,2048]{1,0:T(8,128)(2,1)} %all-gather.7.cloned.1.call-done, pred[2048]{0:T(1024)(128)(4,1)S(1)} %broadcast_compare_fusion.2, bf16[2,2048,512]{2,1,0:T(8,128)(2,1)} %param.16), kind=kOutput, calls=%fused_computation.80 | convolution fusion | flops 4297064448 | bytes 12584960 | tf_op jit(solution)/shard_map/td,df->tf/dot_general | solution.py:21
  72.2 5.8 %select_convert_fusion.5 = bf16[2048,512]{1,0:T(8,128)(2,1)} fusion(bf16[2048,2048]{1,0:T(8,128)(2,1)S(1)} %copy-done.31, pred[2048]{0:T(1024)(128)(4,1)S(1)} %broadcast_compare_fusion.2, bf16[2,2048,512]{2,1,0:T(8,128)(2,1)S(1)} %copy-done.10), kind=kOutput, calls=%fused_computation.81 | convolution fusion | flops 4297064448 | bytes 12584960 | tf_op jit(solution)/shard_map/td,df->tf/dot_general | solution.py:21
  78.0 33.2 %all-gather.5.cloned.1.call-done = bf16[2048,2048]{1,0:T(8,128)(2,1)} async-done(((bf16[256,2048]{1,0:T(8,128)(2,1)}), bf16[2048,2048]{1,0:T(8,128)(2,1)}) %all-gather.5.cloned.1.call-update) | async-done | bytes 8388624 | tf_op jit(solution)/shard_map/all_gather | solution.py:60
  111.2 11.0 %fusion.10 = (bf16[2048,512]{1,0:T(8,128)(2,1)S(1)}, f32[2048,512]{1,0:T(8,128)}) fusion(bf16[2048,512]{1,0:T(8,128)(2,1)} %select_convert_fusion.5, bf16[2048,512]{1,0:T(8,128)(2,1)} %select_convert_fusion.4, bf16[2,512,2048]{2,1,0:T(8,128)(2,1)} %param.18, bf16[2048,2048]{1,0:T(8,128)(2,1)} %all-gather.5.cloned.1.call-done, ...), kind=kOutput, calls=%fused_computation.39 | convolution fusion | flops 4320133120 | bytes 20979712 | tf_op jit(solution)/shard_map/td,fd->tf/dot_general | solution.py:21
  122.2 1.3 copy-done.41
  123.5 8.2 %fusion.64 = f32[2048,2048]{1,0:T(8,128)} fusion(bf16[2048,512]{1,0:T(8,128)(2,1)S(1)} %get-tuple-element.70, bf16[2,2048,512]{2,1,0:T(8,128)(2,1)S(1)} %copy-done.34), kind=kOutput, calls=%fused_computation.99 | convolution fusion | flops 4294967296 | bytes 20971520 | tf_op jit(solution)/shard_map/tf,df->td/dot_general | solution.py:21
  131.7 9.4 %select_convert_fusion.6 = bf16[2048,512]{1,0:T(8,128)(2,1)} fusion(bf16[2048,2048]{1,0:T(8,128)(2,1)} %all-gather.7.cloned.1.call-done, pred[2048]{0:T(1024)(128)(4,1)S(1)} %broadcast_compare_fusion.3, bf16[2,2048,512]{2,1,0:T(8,128)(2,1)S(1)} %copy-done.34), kind=kOutput, calls=%fused_computation.83 | convolution fusion | flops 4297064448 | bytes 12584960 | tf_op jit(solution)/shard_map/td,df->tf/dot_general | solution.py:21
  141.1 5.7 %select_convert_fusion.7 = bf16[2048,512]{1,0:T(8,128)(2,1)} fusion(bf16[2048,2048]{1,0:T(8,128)(2,1)S(1)} %bitcast.184, pred[2048]{0:T(1024)(128)(4,1)S(1)} %broadcast_compare_fusion.3, bf16[2,2048,512]{2,1,0:T(8,128)(2,1)S(1)} %copy-done.11), kind=kOutput, calls=%fused_computation.84 | convolution fusion | flops 4297064448 | bytes 12584960 | tf_op jit(solution)/shard_map/td,df->tf/dot_general | solution.py:21
  146.9 9.2 %fusion.6 = (bf16[2048,512]{1,0:T(8,128)(2,1)}, f32[2048,512]{1,0:T(8,128)}) fusion(bf16[2048,512]{1,0:T(8,128)(2,1)} %select_convert_fusion.7, bf16[2048,512]{1,0:T(8,128)(2,1)} %select_convert_fusion.6, bf16[2,512,2048]{2,1,0:T(8,128)(2,1)S(1)} %copy-done.32, bf16[2048,2048]{1,0:T(8,128)(2,1)S(1)} %bitcast.180, f32[2048]{0:T(1024)S(1)} %broadcast_select_fusion.3), kind=kOutput, calls=%fused_computation.35 | convolution fusion | flops 4320133120 | bytes 20979712 | tf_op jit(solution)/shard_map/td,fd->tf/dot_general | solution.py:21
  156.1 9.9 %fusion.76 = f32[2048,2048]{1,0:T(8,128)} fusion(bf16[2048,512]{1,0:T(8,128)(2,1)} %get-tuple-element.72, bf16[2,2048,512]{2,1,0:T(8,128)(2,1)S(1)} %copy-done.34), kind=kOutput, calls=%fused_computation.111 | convolution fusion | flops 4294967296 | bytes 20971520 | tf_op jit(solution)/shard_map/tf,df->td/dot_general | solution.py:21
  166.0 8.2 %fusion.82 = f32[2048,2048]{1,0:T(8,128)} fusion(bf16[2,2048,512]{2,1,0:T(8,128)(2,1)S(1)} %copy-done.11, f32[2048,512]{1,0:T(8,128)S(1)} %copy-done.45, bf16[2048,512]{1,0:T(8,128)(2,1)S(1)} %copy-done.49), kind=kOutput, calls=%fused_computation.117 | convolution fusion | flops 4302307328 | bytes 25165824 | tf_op jit(solution)/shard_map/tf,df->td/dot_general | solution.py:21
  174.2 26.2 %reduce-precision_add_fusion.1 = f32[2048,2048]{1,0:T(8,128)} fusion(f32[2048,2048]{1,0:T(8,128)} %fusion.64, f32[2048,2048]{1,0:T(8,128)} %fusion.76, f32[2048,2048]{1,0:T(8,128)} %fusion.82, bf16[2,2048,512]{2,1,0:T(8,128)(2,1)} %param.17, f32[2048,512]{1,0:T(8,128)} %get-tuple-element.71, bf16[2048,512]{1,0:T(8,128)(2,1)} %select_convert_fusion.4), kind=kOutput, calls=%fused_computation.9 | convolution fusion | flops 4323278848 | bytes 75497472 | tf_op jit(solution)/shard_map/tf,df->td/dot_general | solution.py:21
  200.7 9.9 %select_convert_fusion.2 = bf16[2048,512]{1,0:T(8,128)(2,1)} fusion(bf16[2048,2048]{1,0:T(8,128)(2,1)} %all-gather.11.cloned.1.call-done, pred[2048]{0:T(1024)(128)(4,1)S(1)} %broadcast_compare_fusion.1, bf16[2,2048,512]{2,1,0:T(8,128)(2,1)} %param.16), kind=kOutput, calls=%fused_computation.77 | convolution fusion | flops 4297064448 | bytes 12584960 | tf_op jit(solution)/shard_map/td,df->tf/dot_general | solution.py:21
  210.6 6.0 %select_convert_fusion.3 = bf16[2048,512]{1,0:T(8,128)(2,1)} fusion(bf16[2048,2048]{1,0:T(8,128)(2,1)S(1)} %copy-done.1, pred[2048]{0:T(1024)(128)(4,1)S(1)} %broadcast_compare_fusion.1, bf16[2,2048,512]{2,1,0:T(8,128)(2,1)S(1)} %copy-done.12), kind=kOutput, calls=%fused_computation.78 | convolution fusion | flops 4297064448 | bytes 12584960 | tf_op jit(solution)/shard_map/td,df->tf/dot_general | solution.py:21
  216.7 11.0 %fusion.14 = (bf16[2048,512]{1,0:T(8,128)(2,1)S(1)}, f32[2048,512]{1,0:T(8,128)}) fusion(bf16[2048,512]{1,0:T(8,128)(2,1)} %select_convert_fusion.3, bf16[2048,512]{1,0:T(8,128)(2,1)} %select_convert_fusion.2, bf16[2,512,2048]{2,1,0:T(8,128)(2,1)} %param.18, bf16[2048,2048]{1,0:T(8,128)(2,1)} %all-gather.9.cloned.1.call-done, ...), kind=kOutput, calls=%fused_computation.43 | convolution fusion | flops 4320133120 | bytes 20979712 | tf_op jit(solution)/shard_map/td,fd->tf/dot_general | solution.py:21
  227.7 1.3 copy-done.14
  229.0 8.2 %fusion.73 = f32[2048,2048]{1,0:T(8,128)} fusion(bf16[2048,512]{1,0:T(8,128)(2,1)S(1)} %get-tuple-element.68, bf16[2,2048,512]{2,1,0:T(8,128)(2,1)S(1)} %copy-done.35), kind=kOutput, calls=%fused_computation.108 | convolution fusion | flops 4294967296 | bytes 20971520 | tf_op jit(solution)/shard_map/tf,df->td/dot_general | solution.py:21
  237.3 8.1 %select_convert_fusion = bf16[2048,512]{1,0:T(8,128)(2,1)S(1)} fusion(bf16[2048,2048]{1,0:T(8,128)(2,1)} %all-gather.11.cloned.1.call-done, pred[2048]{0:T(1024)(128)(4,1)S(1)} %broadcast_compare_fusion, bf16[2,2048,512]{2,1,0:T(8,128)(2,1)S(1)} %copy-done.35), kind=kOutput, calls=%fused_computation.74 | convolution fusion | flops 4297064448 | bytes 12584960 | tf_op jit(solution)/shard_map/td,df->tf/dot_general | solution.py:21
  245.4 5.6 %select_convert_fusion.1 = bf16[2048,512]{1,0:T(8,128)(2,1)} fusion(bf16[2048,2048]{1,0:T(8,128)(2,1)S(1)} %bitcast.146, pred[2048]{0:T(1024)(128)(4,1)S(1)} %broadcast_compare_fusion, bf16[2,2048,512]{2,1,0:T(8,128)(2,1)S(1)} %copy-done.13), kind=kOutput, calls=%fused_computation.75 | convolution fusion | flops 4297064448 | bytes 12584960 | tf_op jit(solution)/shard_map/td,df->tf/dot_general | solution.py:21
  251.1 8.6 %fusion.18 = (bf16[2048,512]{1,0:T(8,128)(2,1)S(1)}, f32[2048,512]{1,0:T(8,128)}) fusion(bf16[2048,512]{1,0:T(8,128)(2,1)} %select_convert_fusion.1, bf16[2048,512]{1,0:T(8,128)(2,1)S(1)} %select_convert_fusion, bf16[2,512,2048]{2,1,0:T(8,128)(2,1)S(1)} %copy-done.33, bf16[2048,2048]{1,0:T(8,128)(2,1)S(1)} %bitcast.188, f32[2048]{0:T(1024)S(1)} %broadcast_select_fusion), kind=kOutput, calls=%fused_computation.47 | convolution fusion | flops 4320133120 | bytes 20979712 | tf_op jit(solution)/shard_map/td,fd->tf/dot_general | solution.py:21
  259.7 10.5 %fusion.61 = f32[2048,2048]{1,0:T(8,128)} fusion(bf16[2048,512]{1,0:T(8,128)(2,1)S(1)} %get-tuple-element.66, bf16[2,2048,512]{2,1,0:T(8,128)(2,1)} %param.16), kind=kOutput, calls=%fused_computation.96 | convolution fusion | flops 4294967296 | bytes 20971520 | tf_op jit(solution)/shard_map/tf,df->td/dot_general | solution.py:21
  270.2 8.3 %fusion.79 = f32[2048,2048]{1,0:T(8,128)} fusion(bf16[2,2048,512]{2,1,0:T(8,128)(2,1)S(1)} %copy-done.13, f32[2048,512]{1,0:T(8,128)S(1)} %copy-done.47, bf16[2048,512]{1,0:T(8,128)(2,1)S(1)} %copy-done.52), kind=kOutput, calls=%fused_computation.114 | convolution fusion | flops 4302307328 | bytes 25165824 | tf_op jit(solution)/shard_map/tf,df->td/dot_general | solution.py:21
  278.6 26.3 %reduce-precision_add_fusion = f32[2048,2048]{1,0:T(8,128)} fusion(f32[2048,2048]{1,0:T(8,128)} %fusion.61, f32[2048,2048]{1,0:T(8,128)} %fusion.73, f32[2048,2048]{1,0:T(8,128)} %fusion.79, bf16[2,2048,512]{2,1,0:T(8,128)(2,1)} %param.17, f32[2048,512]{1,0:T(8,128)} %get-tuple-element.67, bf16[2048,512]{1,0:T(8,128)(2,1)} %copy-done.7), kind=kOutput, calls=%fused_computation.8 | convolution fusion | flops 4323278848 | bytes 75497472 | tf_op jit(solution)/shard_map/tf,df->td/dot_general | solution.py:21
  305.0 3.0 convolution_convert_fusion
  308.1 1.3 convolution_convert_fusion.1
  309.3 0.5 copy-done.18
  309.8 0.6 copy-done.36
  310.5 1.5 fusion.109
  312.0 1.0 copy-done.38
  313.0 3.4 convolution_bitcast_fusion.1
  316.4 5.3 %copy.29 = f32[1,2048,512]{2,1,0:T(8,128)} copy(f32[1,2048,512]{1,2,0:T(8,128)} %convolution_bitcast_fusion.1) | data formatting | bytes 8388608
  321.7 4.9 %convolution_bitcast_fusion.2 = f32[1,2048,512]{1,2,0:T(8,128)} fusion(bf16[512,512]{1,0:T(8,128)(2,1)S(1)} %get-tuple-element.74, bf16[512,2048]{1,0:T(8,128)(2,1)} %param.11), kind=kOutput, calls=%fused_computation.95 | convolution fusion | flops 1073741824 | bytes 6815744 | tf_op jit(solution)/shard_map/td,tf->df/dot_general | solution.py:21
  326.6 5.3 %copy.28 = f32[1,2048,512]{2,1,0:T(8,128)} copy(f32[1,2048,512]{1,2,0:T(8,128)} %convolution_bitcast_fusion.2) | data formatting | bytes 8388608
  331.9 3.4 fusion.137
  335.4 3.6 convolution_bitcast_fusion
  338.9 0.5 slice-done.13
  339.4 1.7 copy-done.46
  341.2 6.3 %fusion.131 = f32[512,2048]{1,0:T(8,128)} fusion(bf16[2048,2048]{1,0:T(8,128)(2,1)S(1)} %bitcast.186, f32[2048,512]{1,0:T(8,128)S(1)} %copy-done.46, bf16[2048,512]{1,0:T(8,128)(2,1)S(1)} %copy-done.50), kind=kOutput, calls=%fused_computation.206 | convolution fusion | flops 4302307328 | bytes 18874368 | tf_op jit(solution)/shard_map/td,tf->df/dot_general | solution.py:21
  347.5 6.9 %fusion.132 = f32[512,2048]{1,0:T(8,128)} fusion(bf16[2048,2048]{1,0:T(8,128)(2,1)S(1)} %bitcast.186, f32[2048,512]{1,0:T(8,128)S(1)} %copy-done.2, bf16[2048,512]{1,0:T(8,128)(2,1)S(1)} %copy-done.5), kind=kOutput, calls=%fused_computation.207 | convolution fusion | flops 4302307328 | bytes 18874368 | tf_op jit(solution)/shard_map/td,tf->df/dot_general | solution.py:21
  354.4 6.8 %add_bitcast_fusion.3 = f32[1,2048,512]{1,2,0:T(8,128)S(1)} fusion(f32[512,2048]{1,0:T(8,128)} %fusion.131, bf16[2048,2048]{1,0:T(8,128)(2,1)S(1)} %bitcast.148, f32[2048,512]{1,0:T(8,128)S(1)} %copy-done.48, bf16[2048,512]{1,0:T(8,128)(2,1)S(1)} %copy-done.53), kind=kOutput, calls=%fused_computation.70 | convolution fusion | flops 4303355904 | bytes 23068672 | tf_op jit(solution)/shard_map/td,tf->df/dot_general | solution.py:21
  361.2 6.6 %add_bitcast_fusion.2 = f32[1,2048,512]{1,2,0:T(8,128)S(1)} fusion(f32[512,2048]{1,0:T(8,128)} %fusion.132, bf16[2048,2048]{1,0:T(8,128)(2,1)S(1)} %bitcast.148, f32[2048,512]{1,0:T(8,128)S(1)} %copy-done.3, bf16[2048,512]{1,0:T(8,128)(2,1)S(1)} %copy-done.8), kind=kOutput, calls=%fused_computation.69 | convolution fusion | flops 4303355904 | bytes 23068672 | tf_op jit(solution)/shard_map/td,tf->df/dot_general | solution.py:21
  367.9 4.0 pad_maximum_fusion.1
  371.8 8.7 %copy.27 = f32[2,2048,512]{2,1,0:T(8,128)} copy(f32[2,2048,512]{1,2,0:T(8,128)} %pad_maximum_fusion.1) | data formatting | bytes 16777216
  380.5 7.7 %fusion.138 = f32[512,2048]{1,0:T(8,128)S(1)} fusion(bf16[2048,512]{1,0:T(8,128)(2,1)} %get-tuple-element.72, bf16[2048,2048]{1,0:T(8,128)(2,1)} %all-gather.7.cloned.1.call-done), kind=kOutput, calls=%fused_computation.213 | convolution fusion | flops 4294967296 | bytes 14680064 | tf_op jit(solution)/shard_map/td,tf->df/dot_general | solution.py:21
  388.3 7.4 %fusion.139 = f32[512,2048]{1,0:T(8,128)S(1)} fusion(bf16[2048,512]{1,0:T(8,128)(2,1)S(1)} %copy-done.42, bf16[2048,2048]{1,0:T(8,128)(2,1)} %all-gather.7.cloned.1.call-done), kind=kOutput, calls=%fused_computation.214 | convolution fusion | flops 4294967296 | bytes 14680064 | tf_op jit(solution)/shard_map/td,tf->df/dot_general | solution.py:21
  395.7 4.6 add_bitcast_fusion.5
  400.4 4.6 add_bitcast_fusion.4
  405.0 4.0 pad_maximum_fusion
  409.0 8.9 %copy.26 = f32[2,2048,512]{2,1,0:T(8,128)} copy(f32[2,2048,512]{1,2,0:T(8,128)} %pad_maximum_fusion) | data formatting | bytes 16777216
  417.9 12.3 %fusion.41 = f32[512,2048]{1,0:T(8,128)} fusion(bf16[2048,2048]{1,0:T(8,128)(2,1)} %all-gather.9.cloned.1.call-done, f32[2048]{0:T(1024)S(1)} %copy-done.30, bf16[2048,512]{1,0:T(8,128)(2,1)} %select_convert_fusion.3, bf16[2048,512]{1,0:T(8,128)(2,1)} %select_convert_fusion.2), kind=kOutput, calls=%fused_computation.87 | convolution fusion | flops 4315938816 | bytes 16785408 | tf_op jit(solution)/shard_map/tf,td->fd/dot_general | solution.py:21
  430.2 11.2 %fusion.37 = f32[512,2048]{1,0:T(8,128)} fusion(bf16[2048,2048]{1,0:T(8,128)(2,1)} %all-gather.9.cloned.1.call-done, f32[2048]{0:T(1024)S(1)} %copy-done.28, bf16[2048,512]{1,0:T(8,128)(2,1)S(1)} %copy-done.55, bf16[2048,512]{1,0:T(8,128)(2,1)S(1)} %copy-done.9), kind=kOutput, calls=%fused_computation.85 | convolution fusion | flops 4315938816 | bytes 16785408 | tf_op jit(solution)/shard_map/tf,td->fd/dot_general | solution.py:21
  441.4 9.2 %add_bitcast_fusion.1 = f32[1,512,2048]{2,1,0:T(8,128)S(1)} fusion(f32[512,2048]{1,0:T(8,128)} %fusion.41, bf16[2048,2048]{1,0:T(8,128)(2,1)S(1)} %bitcast.182, f32[2048]{0:T(1024)S(1)} %copy-done.26, bf16[2048,512]{1,0:T(8,128)(2,1)} %select_convert_fusion.7, bf16[2048,512]{1,0:T(8,128)(2,1)S(1)} %copy-done.51), kind=kOutput, calls=%fused_computation.68 | convolution fusion | flops 4316987392 | bytes 20979712 | tf_op jit(solution)/shard_map/tf,td->fd/dot_general | solution.py:21
  450.7 8.2 %add_bitcast_fusion = f32[1,512,2048]{2,1,0:T(8,128)S(1)} fusion(f32[512,2048]{1,0:T(8,128)} %fusion.37, bf16[2048,2048]{1,0:T(8,128)(2,1)S(1)} %bitcast.182, f32[2048]{0:T(1024)S(1)} %copy-done.24, bf16[2048,512]{1,0:T(8,128)(2,1)S(1)} %copy-done.54, bf16[2048,512]{1,0:T(8,128)(2,1)S(1)} %copy-done.6), kind=kOutput, calls=%fused_computation.67 | convolution fusion | flops 4316987392 | bytes 20979712 | tf_op jit(solution)/shard_map/tf,td->fd/dot_general | solution.py:21
  459.0 4.4 pad_maximum_fusion.2
  463.4 6.9 %fusion.36 = bf16[512,2048]{1,0:T(8,128)(2,1)} fusion(f32[256,2048]{1,0:T(8,128)} %reduce-scatter.5.cloned.1.call-done, f32[256,2048]{1,0:T(8,128)} %reduce-scatter.3.cloned.1.call-done, f32[512,2048]{1,0:T(8,128)} %fusion.137, bf16[2048,512]{1,0:T(8,128)(2,1)} %param.20, f32[512,512]{1,0:T(8,128)S(1)} %copy-done.39, bf16[512,512]{1,0:T(8,128)(2,1)} %copy-done.40), kind=kOutput, calls=%fused_computation.66 | convolution fusion | flops 1079771136 | bytes 14155776 | tf_op jit(solution)/shard_map/tf,df->td/dot_general | solution.py:21
  (169 shorter events, 1.0 us)
Async XLA Ops:
  7.2 297.8 %copy-start = (bf16[2048,512]{1,0:T(8,128)(2,1)S(1)}, bf16[2048,512]{1,0:T(8,128)(2,1)}, u32[]{:S(2)}) copy-start(bf16[2048,512]{1,0:T(8,128)(2,1)} %param.19) | copy-start | bytes 6291460
  7.2 55.0 %all-gather.7.cloned.1.call-start = ((), (), s32[]{:S(2)}) async-start(), calls=%async_computation.3 | async-start | bytes 9437184 | tf_op jit(solution)/shard_map/all_gather | solution.py:59
  10.5 4.9 %copy-start.21 = (f32[512,10]{0,1:T(8,128)S(1)}, f32[512,10]{0,1:T(8,128)}, u32[]{:S(2)}) copy-start(f32[512,10]{0,1:T(8,128)} %param.14) | copy-start | bytes 61444
  10.5 4.9 %copy-start.22 = (s32[512,10]{0,1:T(8,128)S(1)}, s32[512,10]{0,1:T(8,128)}, u32[]{:S(2)}) copy-start(s32[512,10]{0,1:T(8,128)} %param.15) | copy-start | bytes 61444
  10.6 100.6 %all-gather.5.cloned.1.call-start = ((), (), s32[]{:S(2)}) async-start(), calls=%async_computation.2 | async-start | bytes 9437184 | tf_op jit(solution)/shard_map/all_gather | solution.py:60
  13.8 186.8 %all-gather.11.cloned.1.call-start = ((), (), s32[]{:S(2)}) async-start(), calls=%async_computation.6 | async-start | bytes 9437184 | tf_op jit(solution)/shard_map/all_gather | solution.py:59
  14.6 202.1 %all-gather.9.cloned.1.call-start = ((), (), s32[]{:S(2)}) async-start(), calls=%async_computation.5 | async-start | bytes 9437184 | tf_op jit(solution)/shard_map/all_gather | solution.py:60
  15.2 448.2 %reduce-scatter.3.cloned.1.call-start = ((), (), s32[]{:S(2)}) async-start(), calls=%async_computation.4 | async-start | bytes 18874368 | tf_op jit(solution)/shard_map/reduce_scatter | solution.py:73
  30.9 115.9 %copy-start.25 = (f32[2048]{0:T(1024)}, f32[2048]{0:T(1024)S(1)}, u32[]{:S(2)}) copy-start(f32[2048]{0:T(1024)S(1)} %broadcast_select_fusion.3) | copy-start | bytes 24580
  31.0 80.2 %copy-start.23 = (f32[2048]{0:T(1024)}, f32[2048]{0:T(1024)S(1)}, u32[]{:S(2)}) copy-start(f32[2048]{0:T(1024)S(1)} %broadcast_select_fusion.2) | copy-start | bytes 24580
  62.2 10.0 %copy-start.10 = (bf16[2,2048,512]{2,1,0:T(8,128)(2,1)S(1)}, bf16[2,2048,512]{2,1,0:T(8,128)(2,1)}, u32[]{:S(2)}) copy-start(bf16[2,2048,512]{2,1,0:T(8,128)(2,1)} %param.17) | copy-start | bytes 12582916
  62.2 10.0 %copy-start.31 = (bf16[2048,2048]{1,0:T(8,128)(2,1)S(1)}, bf16[2048,2048]{1,0:T(8,128)(2,1)}, u32[]{:S(2)}) copy-start(bf16[2048,2048]{1,0:T(8,128)(2,1)} %all-gather.7.cloned.1.call-done) | copy-start | bytes 25165828
  111.2 12.3 %copy-start.34 = (bf16[2,2048,512]{2,1,0:T(8,128)(2,1)S(1)}, bf16[2,2048,512]{2,1,0:T(8,128)(2,1)}, u32[]{:S(2)}) copy-start(bf16[2,2048,512]{2,1,0:T(8,128)(2,1)} %param.16) | copy-start | bytes 12582916
  123.5 17.6 %slice-start.10 = ((s8[8388608]{0:T(1024)(128)(4,1)}), s8[4194304]{0:T(1024)(128)(4,1)S(1)}, s32[]{:S(2)}) async-start(s8[8388608]{0:T(1024)(128)(4,1)} %bitcast.183), calls=%async_computation.18 | async-start | bytes 8388608
  131.7 9.4 %copy-start.11 = (bf16[2,2048,512]{2,1,0:T(8,128)(2,1)S(1)}, bf16[2,2048,512]{2,1,0:T(8,128)(2,1)}, u32[]{:S(2)}) copy-start(bf16[2,2048,512]{2,1,0:T(8,128)(2,1)} %param.17) | copy-start | bytes 12582916
  131.7 9.4 %slice-start.11 = ((s8[8388608]{0:T(1024)(128)(4,1)}), s8[4194304]{0:T(1024)(128)(4,1)S(1)}, s32[]{:S(2)}) async-start(s8[8388608]{0:T(1024)(128)(4,1)} %bitcast.183), calls=%async_computation.19 | async-start | bytes 8388608
  131.7 15.1 %slice-start.6 = ((s8[8388608]{0:T(1024)(128)(4,1)}), s8[4194304]{0:T(1024)(128)(4,1)S(1)}, s32[]{:S(2)}) async-start(s8[8388608]{0:T(1024)(128)(4,1)} %bitcast.179), calls=%async_computation.14 | async-start | bytes 8388608
  141.1 5.7 %slice-start.7 = ((s8[8388608]{0:T(1024)(128)(4,1)}), s8[4194304]{0:T(1024)(128)(4,1)S(1)}, s32[]{:S(2)}) async-start(s8[8388608]{0:T(1024)(128)(4,1)} %bitcast.179), calls=%async_computation.15 | async-start | bytes 8388608
  141.1 5.7 %copy-start.32 = (bf16[2,512,2048]{2,1,0:T(8,128)(2,1)S(1)}, bf16[2,512,2048]{2,1,0:T(8,128)(2,1)}, u32[]{:S(2)}) copy-start(bf16[2,512,2048]{2,1,0:T(8,128)(2,1)} %param.18) | copy-start | bytes 12582916
  156.1 9.9 %copy-start.45 = (f32[2048,512]{1,0:T(8,128)S(1)}, f32[2048,512]{1,0:T(8,128)}, u32[]{:S(2)}) copy-start(f32[2048,512]{1,0:T(8,128)} %get-tuple-element.73) | copy-start | bytes 12582916
  156.1 9.9 %copy-start.49 = (bf16[2048,512]{1,0:T(8,128)(2,1)S(1)}, bf16[2048,512]{1,0:T(8,128)(2,1)}, u32[]{:S(2)}) copy-start(bf16[2048,512]{1,0:T(8,128)(2,1)} %select_convert_fusion.6) | copy-start | bytes 6291460
  200.5 262.9 %reduce-scatter.5.cloned.1.call-start = ((), (), s32[]{:S(2)}) async-start(), calls=%async_computation.7 | async-start | bytes 18874368 | tf_op jit(solution)/shard_map/reduce_scatter | solution.py:73
  200.6 16.1 %copy-start.29 = (f32[2048]{0:T(1024)}, f32[2048]{0:T(1024)S(1)}, u32[]{:S(2)}) copy-start(f32[2048]{0:T(1024)S(1)} %broadcast_select_fusion.1) | copy-start | bytes 24580
  200.6 50.4 %copy-start.27 = (f32[2048]{0:T(1024)}, f32[2048]{0:T(1024)S(1)}, u32[]{:S(2)}) copy-start(f32[2048]{0:T(1024)S(1)} %broadcast_select_fusion) | copy-start | bytes 24580
  200.7 10.0 %copy-start.1 = (bf16[2048,2048]{1,0:T(8,128)(2,1)S(1)}, bf16[2048,2048]{1,0:T(8,128)(2,1)}, u32[]{:S(2)}) copy-start(bf16[2048,2048]{1,0:T(8,128)(2,1)} %all-gather.11.cloned.1.call-done) | copy-start | bytes 25165828
  200.7 10.0 %copy-start.12 = (bf16[2,2048,512]{2,1,0:T(8,128)(2,1)S(1)}, bf16[2,2048,512]{2,1,0:T(8,128)(2,1)}, u32[]{:S(2)}) copy-start(bf16[2,2048,512]{2,1,0:T(8,128)(2,1)} %param.17) | copy-start | bytes 12582916
  216.7 12.3 %copy-start.35 = (bf16[2,2048,512]{2,1,0:T(8,128)(2,1)S(1)}, bf16[2,2048,512]{2,1,0:T(8,128)(2,1)}, u32[]{:S(2)}) copy-start(bf16[2,2048,512]{2,1,0:T(8,128)(2,1)} %param.16) | copy-start | bytes 12582916
  229.0 16.3 %slice-start = ((s8[8388608]{0:T(1024)(128)(4,1)}), s8[4194304]{0:T(1024)(128)(4,1)S(1)}, s32[]{:S(2)}) async-start(s8[8388608]{0:T(1024)(128)(4,1)} %bitcast.145), calls=%async_computation.8 | async-start | bytes 8388608
  237.2 8.1 %slice-start.1 = ((s8[8388608]{0:T(1024)(128)(4,1)}), s8[4194304]{0:T(1024)(128)(4,1)S(1)}, s32[]{:S(2)}) async-start(s8[8388608]{0:T(1024)(128)(4,1)} %bitcast.145), calls=%async_computation.9 | async-start | bytes 8388608
  237.2 8.1 %copy-start.13 = (bf16[2,2048,512]{2,1,0:T(8,128)(2,1)S(1)}, bf16[2,2048,512]{2,1,0:T(8,128)(2,1)}, u32[]{:S(2)}) copy-start(bf16[2,2048,512]{2,1,0:T(8,128)(2,1)} %param.17) | copy-start | bytes 12582916
  237.3 13.8 %slice-start.14 = ((s8[8388608]{0:T(1024)(128)(4,1)}), s8[4194304]{0:T(1024)(128)(4,1)S(1)}, s32[]{:S(2)}) async-start(s8[8388608]{0:T(1024)(128)(4,1)} %bitcast.187), calls=%async_computation.22 | async-start | bytes 8388608
  245.4 5.7 %copy-start.7 = (bf16[2048,512]{1,0:T(8,128)(2,1)}, bf16[2048,512]{1,0:T(8,128)(2,1)S(1)}, u32[]{:S(2)}) copy-start(bf16[2048,512]{1,0:T(8,128)(2,1)S(1)} %select_convert_fusion) | copy-start | bytes 6291460
  245.4 5.7 %slice-start.15 = ((s8[8388608]{0:T(1024)(128)(4,1)}), s8[4194304]{0:T(1024)(128)(4,1)S(1)}, s32[]{:S(2)}) async-start(s8[8388608]{0:T(1024)(128)(4,1)} %bitcast.187), calls=%async_computation.23 | async-start | bytes 8388608
  245.4 5.7 %copy-start.33 = (bf16[2,512,2048]{2,1,0:T(8,128)(2,1)S(1)}, bf16[2,512,2048]{2,1,0:T(8,128)(2,1)}, u32[]{:S(2)}) copy-start(bf16[2,512,2048]{2,1,0:T(8,128)(2,1)} %param.18) | copy-start | bytes 12582916
  259.7 10.6 %copy-start.16 = (bf16[2048,512]{1,0:T(8,128)(2,1)}, bf16[2048,512]{1,0:T(8,128)(2,1)S(1)}, u32[]{:S(2)}) copy-start(bf16[2048,512]{1,0:T(8,128)(2,1)S(1)} %get-tuple-element.66) | copy-start | bytes 6291460
  259.7 10.6 %copy-start.47 = (f32[2048,512]{1,0:T(8,128)S(1)}, f32[2048,512]{1,0:T(8,128)}, u32[]{:S(2)}) copy-start(f32[2048,512]{1,0:T(8,128)} %get-tuple-element.69) | copy-start | bytes 12582916
  259.7 10.6 %copy-start.52 = (bf16[2048,512]{1,0:T(8,128)(2,1)S(1)}, bf16[2048,512]{1,0:T(8,128)(2,1)}, u32[]{:S(2)}) copy-start(bf16[2048,512]{1,0:T(8,128)(2,1)} %select_convert_fusion.2) | copy-start | bytes 6291460
  308.0 27.3 %copy-start.40 = (bf16[512,512]{1,0:T(8,128)(2,1)}, bf16[512,512]{1,0:T(8,128)(2,1)S(1)}, u32[]{:S(2)}) copy-start(bf16[512,512]{1,0:T(8,128)(2,1)S(1)} %convolution_convert_fusion) | copy-start | bytes 1572868
  331.9 7.0 %slice-start.12 = ((s8[8388608]{0:T(1024)(128)(4,1)}), s8[4194304]{0:T(1024)(128)(4,1)S(1)}, s32[]{:S(2)}) async-start(s8[8388608]{0:T(1024)(128)(4,1)} %bitcast.185), calls=%async_computation.20 | async-start | bytes 8388608
  331.9 7.0 %copy-start.50 = (bf16[2048,512]{1,0:T(8,128)(2,1)S(1)}, bf16[2048,512]{1,0:T(8,128)(2,1)}, u32[]{:S(2)}) copy-start(bf16[2048,512]{1,0:T(8,128)(2,1)} %select_convert_fusion.6) | copy-start | bytes 6291460
  335.4 5.8 %copy-start.46 = (f32[2048,512]{1,0:T(8,128)S(1)}, f32[2048,512]{1,0:T(8,128)}, u32[]{:S(2)}) copy-start(f32[2048,512]{1,0:T(8,128)} %get-tuple-element.73) | copy-start | bytes 12582916
  341.2 6.3 %copy-start.2 = (f32[2048,512]{1,0:T(8,128)S(1)}, f32[2048,512]{1,0:T(8,128)}, u32[]{:S(2)}) copy-start(f32[2048,512]{1,0:T(8,128)} %get-tuple-element.71) | copy-start | bytes 12582916
  341.2 6.3 %copy-start.5 = (bf16[2048,512]{1,0:T(8,128)(2,1)S(1)}, bf16[2048,512]{1,0:T(8,128)(2,1)}, u32[]{:S(2)}) copy-start(bf16[2048,512]{1,0:T(8,128)(2,1)} %select_convert_fusion.4) | copy-start | bytes 6291460
  341.2 13.2 %slice-start.2 = ((s8[8388608]{0:T(1024)(128)(4,1)}), s8[4194304]{0:T(1024)(128)(4,1)S(1)}, s32[]{:S(2)}) async-start(s8[8388608]{0:T(1024)(128)(4,1)} %bitcast.147), calls=%async_computation.10 | async-start | bytes 8388608
  347.5 6.9 %slice-start.3 = ((s8[8388608]{0:T(1024)(128)(4,1)}), s8[4194304]{0:T(1024)(128)(4,1)S(1)}, s32[]{:S(2)}) async-start(s8[8388608]{0:T(1024)(128)(4,1)} %bitcast.147), calls=%async_computation.11 | async-start | bytes 8388608
  347.5 6.9 %copy-start.48 = (f32[2048,512]{1,0:T(8,128)S(1)}, f32[2048,512]{1,0:T(8,128)}, u32[]{:S(2)}) copy-start(f32[2048,512]{1,0:T(8,128)} %get-tuple-element.69) | copy-start | bytes 12582916
  347.5 6.9 %copy-start.53 = (bf16[2048,512]{1,0:T(8,128)(2,1)S(1)}, bf16[2048,512]{1,0:T(8,128)(2,1)}, u32[]{:S(2)}) copy-start(bf16[2048,512]{1,0:T(8,128)(2,1)} %select_convert_fusion.2) | copy-start | bytes 6291460
  354.4 6.8 %copy-start.3 = (f32[2048,512]{1,0:T(8,128)S(1)}, f32[2048,512]{1,0:T(8,128)}, u32[]{:S(2)}) copy-start(f32[2048,512]{1,0:T(8,128)} %get-tuple-element.67) | copy-start | bytes 12582916
  354.4 6.8 %copy-start.8 = (bf16[2048,512]{1,0:T(8,128)(2,1)S(1)}, bf16[2048,512]{1,0:T(8,128)(2,1)}, u32[]{:S(2)}) copy-start(bf16[2048,512]{1,0:T(8,128)(2,1)} %copy-done.7) | copy-start | bytes 6291460
  380.5 7.7 %copy-start.42 = (bf16[2048,512]{1,0:T(8,128)(2,1)S(1)}, bf16[2048,512]{1,0:T(8,128)(2,1)}, u32[]{:S(2)}) copy-start(bf16[2048,512]{1,0:T(8,128)(2,1)} %copy-done.41) | copy-start | bytes 6291460
  380.5 15.2 %slice-start.4 = ((s8[8388608]{0:T(1024)(128)(4,1)}), s8[4194304]{0:T(1024)(128)(4,1)S(1)}, s32[]{:S(2)}) async-start(s8[8388608]{0:T(1024)(128)(4,1)} %bitcast.149), calls=%async_computation.12 | async-start | bytes 8388608
  388.3 7.5 %slice-start.5 = ((s8[8388608]{0:T(1024)(128)(4,1)}), s8[4194304]{0:T(1024)(128)(4,1)S(1)}, s32[]{:S(2)}) async-start(s8[8388608]{0:T(1024)(128)(4,1)} %bitcast.149), calls=%async_computation.13 | async-start | bytes 8388608
  388.3 7.5 %copy-start.15 = (bf16[2048,512]{1,0:T(8,128)(2,1)S(1)}, bf16[2048,512]{1,0:T(8,128)(2,1)}, u32[]{:S(2)}) copy-start(bf16[2048,512]{1,0:T(8,128)(2,1)} %copy-done.14) | copy-start | bytes 6291460
  409.0 8.9 %copy-start.30 = (f32[2048]{0:T(1024)S(1)}, f32[2048]{0:T(1024)}, u32[]{:S(2)}) copy-start(f32[2048]{0:T(1024)} %copy-done.29) | copy-start | bytes 24580
  417.8 12.3 %copy-start.9 = (bf16[2048,512]{1,0:T(8,128)(2,1)S(1)}, bf16[2048,512]{1,0:T(8,128)(2,1)}, u32[]{:S(2)}) copy-start(bf16[2048,512]{1,0:T(8,128)(2,1)} %copy-done.7) | copy-start | bytes 6291460
  417.9 12.3 %copy-start.28 = (f32[2048]{0:T(1024)S(1)}, f32[2048]{0:T(1024)}, u32[]{:S(2)}) copy-start(f32[2048]{0:T(1024)} %copy-done.27) | copy-start | bytes 24580
  417.9 12.3 %copy-start.55 = (bf16[2048,512]{1,0:T(8,128)(2,1)S(1)}, bf16[2048,512]{1,0:T(8,128)(2,1)}, u32[]{:S(2)}) copy-start(bf16[2048,512]{1,0:T(8,128)(2,1)} %select_convert_fusion.1) | copy-start | bytes 6291460
  417.9 23.5 %slice-start.8 = ((s8[8388608]{0:T(1024)(128)(4,1)}), s8[4194304]{0:T(1024)(128)(4,1)S(1)}, s32[]{:S(2)}) async-start(s8[8388608]{0:T(1024)(128)(4,1)} %bitcast.181), calls=%async_computation.16 | async-start | bytes 8388608
  430.2 11.2 %copy-start.26 = (f32[2048]{0:T(1024)S(1)}, f32[2048]{0:T(1024)}, u32[]{:S(2)}) copy-start(f32[2048]{0:T(1024)} %copy-done.25) | copy-start | bytes 24580
  430.2 11.2 %slice-start.9 = ((s8[8388608]{0:T(1024)(128)(4,1)}), s8[4194304]{0:T(1024)(128)(4,1)S(1)}, s32[]{:S(2)}) async-start(s8[8388608]{0:T(1024)(128)(4,1)} %bitcast.181), calls=%async_computation.17 | async-start | bytes 8388608
  430.2 11.2 %copy-start.51 = (bf16[2048,512]{1,0:T(8,128)(2,1)S(1)}, bf16[2048,512]{1,0:T(8,128)(2,1)}, u32[]{:S(2)}) copy-start(bf16[2048,512]{1,0:T(8,128)(2,1)} %select_convert_fusion.6) | copy-start | bytes 6291460
  441.4 9.3 %copy-start.6 = (bf16[2048,512]{1,0:T(8,128)(2,1)S(1)}, bf16[2048,512]{1,0:T(8,128)(2,1)}, u32[]{:S(2)}) copy-start(bf16[2048,512]{1,0:T(8,128)(2,1)} %select_convert_fusion.4) | copy-start | bytes 6291460
  441.4 9.3 %copy-start.24 = (f32[2048]{0:T(1024)S(1)}, f32[2048]{0:T(1024)}, u32[]{:S(2)}) copy-start(f32[2048]{0:T(1024)} %copy-done.23) | copy-start | bytes 24580
  441.4 9.3 %copy-start.54 = (bf16[2048,512]{1,0:T(8,128)(2,1)S(1)}, bf16[2048,512]{1,0:T(8,128)(2,1)}, u32[]{:S(2)}) copy-start(bf16[2048,512]{1,0:T(8,128)(2,1)} %select_convert_fusion.5) | copy-start | bytes 6291460
  (14 other events, 40.2 us)
Sparse Core Ops, SparseCore 0:
  10.7 51.4 all-gather.6
  64.4 46.7 all-gather.4
  113.4 46.6 all-gather.10
  162.1 46.6 all-gather.8
  211.0 88.0 reduce-scatter.2
  305.1 88.0 reduce-scatter.4

commit v2 on v0

v2 whole, which is shorter than its diff:
```python
import functools

import jax
import jax.numpy as jnp
from jax import lax
from jax.experimental import pallas as pl
from jax.experimental.pallas import tpu as pltpu
from jax.sharding import PartitionSpec as P

CW = 256
F32, BF16 = jnp.float32, jnp.bfloat16
MESH = pl.DeviceIdType.MESH
NN = (((1,), (0,)), ((), ()))
NT = (((1,), (1,)), ((), ()))


def dot(a, b, dims):
    return lax.dot_general(a, b, dims, preferred_element_type=F32)


def moe_kernel(tok, dim, ff, cw, x_loc, dy_loc, gt, w1, w3, w2, s1, s3, s2,
               gx, dw1, dw3, dw2, sw1, sw3, sw2, x_all, dy_all, z_all, pp, q_sum, rsh, from_l, from_r, opp,
               w1v, w3v, w2v, act, xt, dyt, zt, dat, dbt, acc, xc, tmp, gall,
               wsem, gsend, grecv, ssem, rsem, psend, precv, r1s, r1r, r2s, r2r, r3s, r3r, lsem, xcs, o1s, o2s, gxs):
    me = lax.axis_index("ep")
    core = lax.rem(me, 2)
    xpos = me // 2
    right = 2 * lax.rem(xpos + 1, 4) + core
    left = 2 * lax.rem(xpos + 3, 4) + core
    far = 2 * lax.rem(xpos + 2, 4) + core
    mate = 2 * xpos + 1 - core
    half = tok // 2
    rows = tok // 8

    def remote(src, dst, send, recv, dev):
        return pltpu.make_async_remote_copy(src_ref=src, dst_ref=dst, send_sem=send, recv_sem=recv, device_id={"ep": dev}, device_id_type=MESH)

    def local(src, dst, sem):
        return pltpu.make_async_copy(src, dst, sem)

    def o1(b, h):
        return acc.at[b, pl.ds(0, cw), pl.ds((1 + h) * ff, ff)]

    def o2(b, e):
        return acc.at[b, pl.ds(0, ff), pl.ds(e * cw, cw)]

    def load(k, b, s, ref):
        return local(s, ref.at[b], wsem.at[k, b])

    barrier = pltpu.get_barrier_semaphore()
    for d in range(1, 8):
        pl.semaphore_signal(barrier, inc=1, device_id={"ep": lax.rem(me + d, 8)}, device_id_type=MESH)

    shared_loads = [load(0, 1, s1, w1v), load(1, 1, s3, w3v), load(2, 1, s2, w2v)]
    first_loads = [load(0, 0, w1.at[0], w1v), load(1, 0, w3.at[0], w3v), load(2, 0, w2.at[0], w2v)]
    second_loads = [load(0, 1, w1.at[1], w1v), load(1, 1, w3.at[1], w3v), load(2, 1, w2.at[1], w2v)]
    own_loads = [local(x_loc, xt, lsem.at[0]), local(dy_loc, dyt, lsem.at[1])]
    for c in own_loads + shared_loads + first_loads:
        c.start()
    pl.semaphore_wait(barrier, 7)

    def block(ref, slot):
        return ref.at[pl.ds(pl.multiple_of(slot * tok, tok), tok), :]

    gates = []
    for d in range(1, 8):
        peer = lax.rem(me + d, 8)
        gates.append(remote(gt.at[peer], gall.at[me], gsend.at[d], grecv.at[me], peer))
        gates[-1].start()
    own_gate = local(gt.at[me], gall.at[me], lsem.at[2])
    own_gate.start()

    def message(k):
        src_dst = [
            (x_loc, x_all, me, right), (dy_loc, dy_all, me, right), (dy_loc, dy_all, me, left), (x_loc, x_all, me, left),
            (x_loc, x_all, me, mate), (dy_loc, dy_all, me, mate),
            (None, x_all, left, right), (None, dy_all, right, left),
            (None, x_all, left, mate), (None, dy_all, left, mate), (None, x_all, right, mate), (None, dy_all, right, mate),
            (None, x_all, far, mate), (None, dy_all, far, mate),
        ][k]
        src, dst, slot, dev = src_dst
        return remote(block(dst, slot) if src is None else src, block(dst, slot), ssem.at[k], rsem.at[k], dev)

    for k in (4, 5, 0, 2, 1, 3):
        message(k).start()

    def forward(col, wb, ab, routed, gate_row, ab_out, before_sum):
        if routed:
            gate = jnp.transpose(jnp.broadcast_to(gate_row, (128, tok)))
            kept = gate < jnp.inf
            gate = jnp.where(kept, gate, 0.0)
            for n in range(dim // 128):
                s = slice(n * 128, (n + 1) * 128)
                zt[:, s] = (dyt[:, s].astype(F32) * gate).astype(BF16)
            wide = jnp.concatenate([kept] * (cw // 128), axis=1)
            dz = zt
        else:
            dz = dyt
        for n in range(ff // cw):
            s = slice(n * cw, (n + 1) * cw)
            a = dot(xt[...], w1v[wb, :, s], NN)
            b = dot(xt[...], w3v[wb, :, s], NN)
            if routed:
                a = jnp.where(wide, a, 0.0)
                b = jnp.where(wide, b, 0.0)
            a = a.astype(BF16).astype(F32)
            b = b.astype(BF16).astype(F32)
            g = dot(dz[...], w2v[wb, s, :], NT)
            sig = jax.nn.sigmoid(a)
            silu = a * sig
            hid = (silu * b).astype(BF16)
            da = (g * b * sig * (1.0 + a * (1.0 - sig))).astype(BF16)
            db = (g * silu).astype(BF16)
            dat[:, s] = da
            dbt[:, s] = db
            act[ab, 0, s, pl.ds(col, tok)] = jnp.transpose(hid)
            act[ab, 1, s, pl.ds(col, tok)] = jnp.transpose(da)
            act[ab, 2, s, pl.ds(col, tok)] = jnp.transpose(db)
        before_sum()
        for n in range(dim // cw):
            s = slice(n * cw, (n + 1) * cw)
            r = dot(dat[...], w1v[wb, s, :], NT) + dot(dbt[...], w3v[wb, s, :], NT)
            if routed:
                acc[ab_out, :, s] += r.astype(BF16).astype(F32)
            else:
                acc[ab_out, :, s] = r

    for c in own_loads + shared_loads:
        c.wait()
    keep = [local(xt, block(x_all, me), lsem.at[0]), local(dyt, block(dy_all, me), lsem.at[1])]
    for c in keep:
        c.start()
    forward(0, 1, 1, False, None, 1, lambda: None)
    for c in second_loads:
        c.start()
    save = local(acc.at[1], rsh, lsem.at[3])
    save.start()

    def shared_grads(n, _):
        s = pl.ds(pl.multiple_of(n * cw, cw), cw)
        outs = [local(o1(0, 0), sw1.at[s, :], o1s.at[0]), local(o1(0, 1), sw3.at[s, :], o1s.at[1]), local(o2(0, 0), sw2.at[:, s], o2s.at[0])]

        @pl.when(n > 0)
        def _():
            for c in outs:
                c.wait()
        o1(0, 0)[...] = jnp.transpose(dot(act[1, 1, :, 0:tok], xt[:, s], NN))
        o1(0, 1)[...] = jnp.transpose(dot(act[1, 2, :, 0:tok], xt[:, s], NN))
        o2(0, 0)[...] = dot(act[1, 0, :, 0:tok], dyt[:, s], NN)
        for c in outs:
            c.start()
        return 0

    lax.fori_loop(0, dim // cw, shared_grads, 0)
    local(o1(0, 0), sw1.at[pl.ds(0, cw), :], o1s.at[0]).wait()
    local(o1(0, 1), sw3.at[pl.ds(0, cw), :], o1s.at[1]).wait()
    local(o2(0, 0), sw2.at[:, pl.ds(0, cw)], o2s.at[0]).wait()
    save.wait()
    for c in keep + first_loads + second_loads + [own_gate]:
        c.wait()
    for d in range(1, 8):
        peer = lax.rem(me + d, 8)
        remote(gt.at[peer], gall.at[peer], gsend.at[d], grecv.at[peer], peer).wait_recv()

    def phase1(to_left):
        if to_left:
            return remote(q_sum.at[1, pl.ds(0, half), :], from_r.at[pl.ds(0, half), :], r1s.at[0], r1r.at[0], left)
        return remote(q_sum.at[2, pl.ds(half, half), :], from_l.at[pl.ds(half, half), :], r1s.at[1], r1r.at[1], right)

    def phase2(k, to_left):
        if to_left:
            s = pl.ds(half + k * rows, rows)
            return remote(q_sum.at[3, s, :], opp.at[s, :], r2s.at[0, k], r2r.at[0, k], left)
        s = pl.ds(k * rows, rows)
        return remote(q_sum.at[3, s, :], opp.at[s, :], r2s.at[1, k], r2r.at[1, k], right)

    def phase3(k, to_left):
        if to_left:
            s = pl.ds(pl.multiple_of(half + k * rows, rows), rows)
            return remote(acc.at[0, s, :], from_r.at[s, :], r3s.at[0, k], r3r.at[0, k], left)
        s = pl.ds(pl.multiple_of(k * rows, rows), rows)
        return remote(acc.at[0, s, :], from_l.at[s, :], r3s.at[1, k], r3r.at[1, k], right)

    def partial(i):
        return remote(acc.at[0], pp.at[i], psend.at[i], precv.at[i], mate)

    def tile(j, _):
        i = jnp.where(j < 2, 0, jnp.where(j >= 6, 3, 1 + lax.rem(j, 2)))
        t = jnp.where(j < 2, j, jnp.where(j >= 6, j - 6, (j - 2) // 2))
        off = jnp.where(i == 1, 3, jnp.where(i == 2, 1, jnp.where(i == 3, 2, 0)))
        slot = 2 * lax.rem(xpos + off, 4) + jnp.where(t == 0, 1 - core, core)

        @pl.when(j == 0)
        def _():
            message(4).wait_recv()
            message(5).wait_recv()

        @pl.when(j == 2)
        def _():
            for k, outs in ((0, (6, 8)), (2, (7, 11)), (1, (9,)), (3, (10,))):
                message(k).wait_recv()
                for o in outs:
                    message(o).start()
            message(8).wait_recv()
            message(9).wait_recv()

        @pl.when(j == 3)
        def _():
            message(10).wait_recv()
            message(11).wait_recv()

        @pl.when(j == 6)
        def _():
            message(6).wait_recv()
            message(12).start()
            message(7).wait_recv()
            message(13).start()
            message(12).wait_recv()
            message(13).wait_recv()

        loads = [local(block(x_all, slot), xt, lsem.at[0]), local(block(dy_all, slot), dyt, lsem.at[1])]
        for c in loads:
            c.start()
        for c in loads:
            c.wait()
        col = pl.multiple_of(slot * tok, tok)

        def expert(e, _):
            put_z = local(zt, z_all.at[e, pl.ds(col, tok), :], lsem.at[2])

            def before_sum():
                put_z.start()

                @pl.when((e == 0) & (t == 0))
                def _():
                    @pl.when(i > 0)
                    def _():
                        partial(i - 1).wait_send()
                    acc[0] = jnp.zeros((tok, dim), F32)

                @pl.when((e == 0) & (t == 1))
                def _():
                    partial(i).wait_recv()
                    get = local(pp.at[i], acc.at[1], lsem.at[3])
                    get.start()
                    get.wait()

            forward(col, e, e, True, gall[slot, pl.ds(e, 1), :], t, before_sum)
            put_z.wait()
            return 0

        lax.fori_loop(0, 2, expert, 0)

        @pl.when(t == 0)
        def _():
            partial(i).start()

        @pl.when(t == 1)
        def _():
            put = local(acc.at[1], q_sum.at[i], lsem.at[3])
            put.start()
            put.wait()

        @pl.when(j == 4)
        def _():
            phase1(True).start()

        @pl.when(j == 5)
        def _():
            phase1(False).start()

        @pl.when(j == 7)
        def _():
            for k in range(4):
                phase2(k, True).start()
                phase2(k, False).start()
        return 0

    lax.fori_loop(0, 8, tile, 0)
    partial(3).wait_send()

    def combine(k):
        for to_left in (False, True):
            base = half if to_left else 0
            s = pl.ds(pl.multiple_of(base + k * rows, rows), rows)
            b = 0 if to_left else 1
            remote(opp.at[s, :], opp.at[s, :], r2s.at[b, k], r2r.at[b, k], right).wait_recv()
            gets = [local(opp.at[s, :], acc.at[0, s, :], lsem.at[0]), local(q_sum.at[1 if to_left else 2, s, :], tmp.at[0], lsem.at[1])]
            for c in gets:
                c.start()
            for c in gets:
                c.wait()
            acc[0, s, :] += tmp[0]
            phase3(k, to_left).start()

    chunks = dim // cw

    def column(n):
        return pl.ds(pl.multiple_of(n * cw, cw), cw)

    def fetch(kind, n, b):
        src = x_all.at[:, column(n)] if kind == 0 else z_all.at[kind - 1, :, column(n)]
        return local(src, xc.at[b], xcs.at[b])

    fetch(0, 0, 0).start()

    def weight_grads(n, _):
        b0 = lax.rem(3 * n, 2)
        b1 = 1 - b0
        fetch(1, n, b1).start()
        fetch(0, n, b0).wait()
        for e in range(2):
            for h, dst in ((0, dw1), (1, dw3)):
                put = local(o1(1, h), dst.at[e, column(n), :], o1s.at[h])
                if e == 0:
                    @pl.when(n > 0)
                    def _():
                        put.wait()
                else:
                    put.wait()
                o1(1, h)[...] = jnp.transpose(dot(act[e, 1 + h], xc[b0], NN))
                put.start()
        fetch(2, n, b0).start()
        for e in range(2):
            b = b1 if e == 0 else b0
            put = local(o2(1, e), dw2.at[e, :, column(n)], o2s.at[e])
            fetch(1 + e, n, b).wait()
            if e == 1:
                @pl.when(n < chunks - 1)
                def _():
                    fetch(0, n + 1, b1).start()

            @pl.when(n > 0)
            def _():
                put.wait()
            o2(1, e)[...] = dot(act[e, 0], xc[b], NN)
            put.start()

        @pl.when(n >= chunks - 4)
        def _():
            combine(n - (chunks - 4))
        return 0

    lax.fori_loop(0, chunks, weight_grads, 0)

    for h, dst in ((0, dw1), (1, dw3)):
        local(o1(1, h), dst.at[1, column(0), :], o1s.at[h]).wait()
    for e in range(2):
        local(o2(1, e), dw2.at[e, :, column(0)], o2s.at[e]).wait()
    get = local(q_sum.at[0], acc.at[1], lsem.at[2])
    get.start()
    phase1(True).wait_recv()
    phase1(False).wait_recv()
    get.wait()

    def own_rows(k, _):
        s = pl.ds(pl.multiple_of(k * rows, rows), rows)
        first = local(rsh.at[s, :], tmp.at[0], lsem.at[0])
        first.start()

        @pl.when(k < 4)
        def _():
            local(from_r.at[s, :], tmp.at[1], lsem.at[1]).start()

        @pl.when(k >= 4)
        def _():
            local(from_l.at[s, :], tmp.at[1], lsem.at[1]).start()
        first.wait()
        local(from_l.at[s, :], tmp.at[1], lsem.at[1]).wait()
        acc[1, s, :] += tmp[0] + tmp[1]
        return 0

    lax.fori_loop(0, 8, own_rows, 0)

    def last(k):
        sa, sb = pl.ds(k * rows, rows), pl.ds(half + k * rows, rows)
        phase3(k, False).wait_recv()
        ga = local(from_l.at[sa, :], tmp.at[0], lsem.at[0])
        ga.start()
        phase3(k, True).wait_recv()
        gb = local(from_r.at[sb, :], tmp.at[1], lsem.at[1])
        gb.start()
        ga.wait()
        xt[sa, :] = (acc[1, sa, :] + tmp[0]).astype(BF16)
        pa = local(xt.at[sa, :], gx.at[sa, :], gxs.at[0, k])
        pa.start()
        gb.wait()
        xt[sb, :] = (acc[1, sb, :] + tmp[1]).astype(BF16)
        pb = local(xt.at[sb, :], gx.at[sb, :], gxs.at[1, k])
        pb.start()
        return [pa, pb]

    puts = []
    for k in range(4):
        puts += last(k)
    for c in puts:
        c.wait()
    for c in gates:
        c.wait_send()
    for k in range(14):
        message(k).wait_send()
    for to_left in (True, False):
        phase1(to_left).wait_send()
        for k in range(4):
            phase2(k, to_left).wait_send()
            phase3(k, to_left).wait_send()


def moe_call(x, dy, gt, w1, w3, w2, s1, s3, s2):
    tok, dim = x.shape
    ff = w1.shape[2]
    cw = CW
    sds = jax.ShapeDtypeStruct
    outs = [
        sds((tok, dim), BF16), sds((2, dim, ff), F32), sds((2, dim, ff), F32), sds((2, ff, dim), F32),
        sds((dim, ff), F32), sds((dim, ff), F32), sds((ff, dim), F32),
        sds((8 * tok, dim), BF16), sds((8 * tok, dim), BF16), sds((2, 8 * tok, dim), BF16),
        sds((4, tok, dim), F32), sds((4, tok, dim), F32), sds((tok, dim), F32), sds((tok, dim), F32), sds((tok, dim), F32), sds((tok, dim), F32),
    ]
    V, D = pltpu.VMEM, pltpu.SemaphoreType.DMA
    scratch = [
        V((2, dim, ff), BF16), V((2, dim, ff), BF16), V((2, ff, dim), BF16), V((2, 3, ff, 8 * tok), BF16),
        V((tok, dim), BF16), V((tok, dim), BF16), V((tok, dim), BF16), V((tok, ff), BF16), V((tok, ff), BF16),
        V((2, tok, dim), F32), V((2, 8 * tok, cw), BF16), V((2, tok // 8, dim), F32),
        V((8, 8, tok), F32),
        D((3, 2)), D((8,)), D((8,)), D((14,)), D((14,)), D((4,)), D((4,)), D((2,)), D((2,)),
        D((2, 4)), D((2, 4)), D((2, 4)), D((2, 4)), D((4,)), D((2,)), D((2,)), D((2,)), D((2, 4)),
    ]
    any_spec = pl.BlockSpec(memory_space=pl.ANY)
    return pl.pallas_call(
        functools.partial(moe_kernel, tok, dim, ff, cw),
        out_shape=outs,
        in_specs=[any_spec] * 9,
        out_specs=[any_spec] * len(outs),
        scratch_shapes=scratch,
        compiler_params=pltpu.CompilerParams(collective_id=0, has_side_effects=True, vmem_limit_bytes=67043328),
        name="moe_backward",
    )(x, dy, gt, w1, w3, w2, s1, s3, s2)[:7]


def solution(mesh):
    group = mesh.shape['ep']
    token_spec = P(('dp', 'ep'), None)
    expert_spec = P('ep', None, None)
    whole_spec = P(None, None)
    grad_spec = P(('dp', 'ep'), None, None)

    def local_backward(x_tokens, dy_tokens, expert_ids, gate_vals, slot_pos, w_gate, w_up, w_down, shared_gate, shared_up, shared_down):
        tok_count, top_k = expert_ids.shape
        num_experts = w_gate.shape[0] * group
        ids, pos, gates = expert_ids.T, slot_pos.T, gate_vals.T
        experts = jnp.arange(num_experts, dtype=jnp.int32)[:, None]
        table = jnp.full((num_experts, tok_count), jnp.inf, F32)
        for j in range(top_k):
            table = jnp.where((ids[j:j + 1] == experts) & (pos[j:j + 1] >= 0), gates[j:j + 1], table)
        table = jnp.pad(table.reshape(group, -1, tok_count), ((0, 0), (0, 8 - num_experts // group), (0, 0)))
        gx, dw1, dw3, dw2, sw1, sw3, sw2 = moe_call(x_tokens, dy_tokens, table, w_gate, w_up, w_down, shared_gate, shared_up, shared_down)
        return gx, dw1, dw3, dw2, sw1[None], sw3[None], sw2[None]

    return jax.shard_map(local_backward, mesh=mesh, in_specs=(token_spec, token_spec, token_spec, token_spec, token_spec, expert_spec, expert_spec, expert_spec, whole_spec, whole_spec, whole_spec), out_specs=(token_spec, grad_spec, grad_spec, grad_spec, grad_spec, grad_spec, grad_spec), check_vma=False)
```

time: 1520 us -> 396 us (0.26)
  waiting for transfers between devices: 743 us -> 0 us
  local copies, waits for them, and re-layouts: 415 us -> 33 us
  Pallas kernels: 0 us -> 360 us
  matrix products: 250 us -> 0 us
  other arithmetic: 70.1 us -> 1.53 us
  starting transfers between devices: 25.2 us -> 0 us
    all_to_all x3 -> x0, waiting for transfers between devices: 743 us -> none  [the longest x1 273 us: local_backward(): dz_exp = lax.all_to_all(send_dz, 'ep', 0, 1, tiled=True)]
    pallas_call x0 -> x1, Pallas kernels: none -> 360 us  [moe_call(): pl.pallas_call(functools.partial(moe_kernel, tok, dim, ff, cw), out_shape...]
    dot_general x16 -> x0, matrix products: 250 us -> none  [the longest x1 36.6 us: local_backward(): jnp.einsum('erf,edf->erd', grad_up, w_up, preferred_element_type=jnp.floa...]
    gather x4 -> x0, local copies, waits for them, and re-layouts: 243 us -> none  [take_rows(): return jnp.take(rows, row_index, axis=0, mode='fill', fill_value=0)]
    all_to_all x3 -> x0, local copies, waits for them, and re-layouts: 64.7 us -> none  [the longest x1 21.9 us: local_backward(): lax.all_to_all(grad_exp, 'ep', 1, 0, tiled=True)]
    convert_element_type x1 -> x0, local copies, waits for them, and re-layouts: 56.5 us -> none  [local_backward(): (jnp.einsum('erf,edf->erd', grad_gate, w_gate, preferred_element_type=jnp...]
    scatter x2 -> x0, local copies, waits for them, and re-layouts: 38.7 us -> none  [the longest x1 19.4 us: slot_tables(): jnp.zeros((slot_total + 1,), jnp.float32).at[copy_slot]]
    all_to_all x3 -> x0, starting transfers between devices: 25.2 us -> none  [the longest x1 9 us: local_backward(): x_exp = lax.all_to_all(send_x, 'ep', 0, 1, tiled=True)]
  transfers between devices with their start and end apart: 3 -> 0, of which waited for: 3 -> 0; matrix products, arithmetic and copies ran while one was open for 19% -> 0% of each run, Pallas kernels for 0% -> 0%
where the time goes in v2:
time: 396 us; the launch traced here: 395 us
  Pallas kernels  360 us (91%)
  local copies, waits for them, and re-layouts  33 us (8%)
    pallas_call x1, Pallas kernels, moe_call(): pl.pallas_call(functools.partial(moe_kernel, tok, dim, ff, cw), out_shape...  360 us
    unnamed x19, local copies, waits for them, and re-layouts  30.2 us

profile of v2, /device:TPU:81, one launch (start us, length us, event | category | flops | bytes accessed | tf_op | source)
XLA Modules:
  0.0 394.8 jit_solution(6519037783273177613)
XLA Ops:
  0.6 1.2 compare_reduce_fusion.9
  1.9 1.2 fusion
  3.0 1.0 fusion.1
  4.1 0.3 and_select_fusion.9
  4.4 0.7 pad.4.gt
  5.0 359.6 %moe_backward.1 = (bf16[512,2048]{1,0:T(8,128)(2,1)}, f32[2,2048,512]{2,1,0:T(8,128)}, f32[2,2048,512]{2,1,0:T(8,128)}, f32[2,512,2048]{2,1,0:T(8,128)}, f32[204...) custom-call(bf16[512,2048]{1,0:T(8,128)(2,1)} %x_loc.1, ...), custom_call_target="tpu_custom_call" | custom-call | tf_op jit(solution)/shard_map/moe_backward/pallas_call | solution.py:430
  364.6 0.0 slice-start
  364.6 3.3 copy.25
  367.9 0.0 copy-start
  367.9 0.0 slice-start.1
  367.9 8.8 %copy.26 = f32[2,2048,512]{2,1,0:T(8,128)} copy(f32[2,2048,512]{2,1,0:T(8,128)} %get-tuple-element.59) | data formatting | bytes 16777216
  376.8 0.0 copy-done
  376.8 3.4 copy.27
  380.2 0.0 slice-done
  380.2 0.0 slice-done.1
  380.2 0.0 copy-start.3
  380.2 4.3 %copy.28 = f32[2,512,2048]{2,1,0:T(8,128)} copy(f32[2,512,2048]{2,1,0:T(8,128)S(1)} %bitcast.27) | data formatting | bytes 16777216
  384.4 1.0 copy-done.3
  385.4 0.0 copy-start.2
  385.4 2.1 copy.29
  387.5 1.6 copy-done.2
  389.1 0.0 copy-start.1
  389.1 2.1 copy.30
  391.2 1.6 copy-done.1
  392.8 2.0 copy.31
  (2 shorter events, 0.0 us)
Async XLA Ops:
  364.6 15.6 %slice-start = ((s8[8388608]{0:T(1024)(128)(4,1)}), s8[4194304]{0:T(1024)(128)(4,1)S(1)}, s32[]{:S(2)}) async-start(s8[8388608]{0:T(1024)(128)(4,1)} %bitcast.26), calls=%async_computation | async-start | bytes 8388608
  367.9 8.8 %copy-start = (f32[2,2048,512]{2,1,0:T(8,128)S(1)}, f32[2,2048,512]{2,1,0:T(8,128)}, u32[]{:S(2)}) copy-start(f32[2,2048,512]{2,1,0:T(8,128)} %get-tuple-element.60) | copy-start | bytes 25165828
  367.9 12.2 %slice-start.1 = ((s8[8388608]{0:T(1024)(128)(4,1)}), s8[4194304]{0:T(1024)(128)(4,1)S(1)}, s32[]{:S(2)}) async-start(s8[8388608]{0:T(1024)(128)(4,1)} %bitcast.26), calls=%async_computation.1 | async-start | bytes 8388608
  380.2 5.2 %copy-start.3 = (f32[2048,512]{1,0:T(8,128)S(1)}, f32[2048,512]{1,0:T(8,128)}, u32[]{:S(2)}) copy-start(f32[2048,512]{1,0:T(8,128)} %get-tuple-element.18) | copy-start | bytes 12582916
  385.4 3.7 copy-start.2
  389.1 3.7 copy-start.1

commit v3 on v2

--- a/solution.py
+++ b/solution.py
@@ -21,7 +21,7 @@
 def moe_kernel(tok, dim, ff, cw, x_loc, dy_loc, gt, w1, w3, w2, s1, s3, s2,
                gx, dw1, dw3, dw2, sw1, sw3, sw2, x_all, dy_all, z_all, pp, q_sum, rsh, from_l, from_r, opp,
                w1v, w3v, w2v, act, xt, dyt, zt, dat, dbt, acc, xc, tmp, gall,
-               wsem, gsend, grecv, ssem, rsem, psend, precv, r1s, r1r, r2s, r2r, r3s, r3r, lsem, xcs, o1s, o2s, gxs):
+               wsem, gsend, grecv, ssem, rsem, psend, precv, r1s, r1r, r2s, r2r, r3s, r3r, lsem, xcs, zcs, o1s, o2s, gxs):
     me = lax.axis_index("ep")
     core = lax.rem(me, 2)
     xpos = me // 2
@@ -70,21 +70,33 @@
     own_gate = local(gt.at[me], gall.at[me], lsem.at[2])
     own_gate.start()
 
+    plan = [
+        (me, 0, right), (me, 1, left), (me, 1, right), (me, 0, left), (me, None, mate), (left, 0, right), (right, 1, left),
+        (left, 0, mate), (right, 1, mate), (left, 1, mate), (right, 0, mate), (far, 0, mate), (far, 1, mate),
+    ]
+
     def message(k):
-        src_dst = [
-            (x_loc, x_all, me, right), (dy_loc, dy_all, me, right), (dy_loc, dy_all, me, left), (x_loc, x_all, me, left),
-            (x_loc, x_all, me, mate), (dy_loc, dy_all, me, mate),
-            (None, x_all, left, right), (None, dy_all, right, left),
-            (None, x_all, left, mate), (None, dy_all, left, mate), (None, x_all, right, mate), (None, dy_all, right, mate),
-            (None, x_all, far, mate), (None, dy_all, far, mate),
-        ][k]
-        src, dst, slot, dev = src_dst
-        return remote(block(dst, slot) if src is None else src, block(dst, slot), ssem.at[k], rsem.at[k], dev)
-
-    for k in (4, 5, 0, 2, 1, 3):
-        message(k).start()
-
-    def forward(col, wb, ab, routed, gate_row, ab_out, before_sum):
+        slot, part, dev = plan[k]
+        copies = []
+        for a, (own, every) in enumerate(((x_loc, x_all), (dy_loc, dy_all))):
+            first, size = (0, tok) if part is None else (part * half, half)
+            dst = every.at[pl.ds(pl.multiple_of(slot * tok + first, half), size), :]
+            src = own.at[pl.ds(first, size), :] if k < 5 else dst
+            copies.append(remote(src, dst, ssem.at[k, a], rsem.at[k, a], dev))
+        return copies
+
+    def send(k):
+        for c in message(k):
+            c.start()
+
+    def arrived(k):
+        for c in message(k):
+            c.wait_recv()
+
+    for k in (4, 0, 1, 2, 3):
+        send(k)
+
+    def forward(cols, wb, ab, routed, gate_row, ab_out, before_sum):
         if routed:
             gate = jnp.transpose(jnp.broadcast_to(gate_row, (128, tok)))
             kept = gate < jnp.inf
@@ -113,9 +125,10 @@
             db = (g * silu).astype(BF16)
             dat[:, s] = da
             dbt[:, s] = db
-            act[ab, 0, s, pl.ds(col, tok)] = jnp.transpose(hid)
-            act[ab, 1, s, pl.ds(col, tok)] = jnp.transpose(da)
-            act[ab, 2, s, pl.ds(col, tok)] = jnp.transpose(db)
+            for kind, value in enumerate((hid, da, db)):
+                value = jnp.transpose(value)
+                for h in range(2):
+                    act[ab, kind, s, pl.ds(cols[h], half)] = value[:, h * half:(h + 1) * half]
         before_sum()
         for n in range(dim // cw):
             s = slice(n * cw, (n + 1) * cw)
@@ -130,7 +143,7 @@
     keep = [local(xt, block(x_all, me), lsem.at[0]), local(dyt, block(dy_all, me), lsem.at[1])]
     for c in keep:
         c.start()
-    forward(0, 1, 1, False, None, 1, lambda: None)
+    forward((0, half), 1, 1, False, None, 1, lambda: None)
     for c in second_loads:
         c.start()
     save = local(acc.at[1], rsh, lsem.at[3])
@@ -138,7 +151,7 @@
 
     def shared_grads(n, _):
         s = pl.ds(pl.multiple_of(n * cw, cw), cw)
-        outs = [local(o1(0, 0), sw1.at[s, :], o1s.at[0]), local(o1(0, 1), sw3.at[s, :], o1s.at[1]), local(o2(0, 0), sw2.at[:, s], o2s.at[0])]
+        outs = [local(o1(0, 0), sw1.at[s, :], o1s.at[0, 0]), local(o1(0, 1), sw3.at[s, :], o1s.at[0, 1]), local(o2(0, 0), sw2.at[:, s], o2s.at[0, 0])]
 
         @pl.when(n > 0)
         def _():
@@ -152,9 +165,9 @@
         return 0
 
     lax.fori_loop(0, dim // cw, shared_grads, 0)
-    local(o1(0, 0), sw1.at[pl.ds(0, cw), :], o1s.at[0]).wait()
-    local(o1(0, 1), sw3.at[pl.ds(0, cw), :], o1s.at[1]).wait()
-    local(o2(0, 0), sw2.at[:, pl.ds(0, cw)], o2s.at[0]).wait()
+    local(o1(0, 0), sw1.at[pl.ds(0, cw), :], o1s.at[0, 0]).wait()
+    local(o1(0, 1), sw3.at[pl.ds(0, cw), :], o1s.at[0, 1]).wait()
+    local(o2(0, 0), sw2.at[:, pl.ds(0, cw)], o2s.at[0, 0]).wait()
     save.wait()
     for c in keep + first_loads + second_loads + [own_gate]:
         c.wait()
@@ -165,7 +178,7 @@
     def phase1(to_left):
         if to_left:
             return remote(q_sum.at[1, pl.ds(0, half), :], from_r.at[pl.ds(0, half), :], r1s.at[0], r1r.at[0], left)
-        return remote(q_sum.at[2, pl.ds(half, half), :], from_l.at[pl.ds(half, half), :], r1s.at[1], r1r.at[1], right)
+        return remote(q_sum.at[1, pl.ds(half, half), :], from_l.at[pl.ds(half, half), :], r1s.at[1], r1r.at[1], right)
 
     def phase2(k, to_left):
         if to_left:
@@ -185,51 +198,59 @@
         return remote(acc.at[0], pp.at[i], psend.at[i], precv.at[i], mate)
 
     def tile(j, _):
-        i = jnp.where(j < 2, 0, jnp.where(j >= 6, 3, 1 + lax.rem(j, 2)))
-        t = jnp.where(j < 2, j, jnp.where(j >= 6, j - 6, (j - 2) // 2))
-        off = jnp.where(i == 1, 3, jnp.where(i == 2, 1, jnp.where(i == 3, 2, 0)))
-        slot = 2 * lax.rem(xpos + off, 4) + jnp.where(t == 0, 1 - core, core)
+        i = j // 2
+        t = lax.rem(j, 2)
+        mine = jnp.where(t == 0, 1 - core, core)
+        top = 2 * lax.rem(xpos + jnp.where(i == 0, 0, jnp.where(i == 1, 3, jnp.where(i == 2, 1, 2))), 4) + mine
+        low = 2 * lax.rem(xpos + jnp.where(i == 0, 0, jnp.where(i == 1, 1, jnp.where(i == 2, 3, 2))), 4) + mine
+        cols = (pl.multiple_of(top * tok, tok), pl.multiple_of(low * tok + half, half))
 
         @pl.when(j == 0)
         def _():
-            message(4).wait_recv()
-            message(5).wait_recv()
+            arrived(4)
 
         @pl.when(j == 2)
         def _():
-            for k, outs in ((0, (6, 8)), (2, (7, 11)), (1, (9,)), (3, (10,))):
-                message(k).wait_recv()
-                for o in outs:
-                    message(o).start()
-            message(8).wait_recv()
-            message(9).wait_recv()
-
-        @pl.when(j == 3)
-        def _():
-            message(10).wait_recv()
-            message(11).wait_recv()
+            arrived(0)
+            send(5)
+            send(7)
+            arrived(1)
+            send(6)
+            send(8)
+            arrived(7)
+            arrived(8)
+
+        @pl.when(j == 4)
+        def _():
+            arrived(2)
+            send(9)
+            arrived(3)
+            send(10)
+            arrived(9)
+            arrived(10)
 
         @pl.when(j == 6)
         def _():
-            message(6).wait_recv()
-            message(12).start()
-            message(7).wait_recv()
-            message(13).start()
-            message(12).wait_recv()
-            message(13).wait_recv()
-
-        loads = [local(block(x_all, slot), xt, lsem.at[0]), local(block(dy_all, slot), dyt, lsem.at[1])]
+            arrived(5)
+            send(11)
+            arrived(6)
+            send(12)
+            arrived(11)
+            arrived(12)
+
+        loads = [local(every.at[pl.ds(cols[h], half), :], buf.at[pl.ds(h * half, half), :], wsem.at[h, a])
+                 for h in range(2) for a, (every, buf) in enumerate(((x_all, xt), (dy_all, dyt)))]
         for c in loads:
             c.start()
         for c in loads:
             c.wait()
-        col = pl.multiple_of(slot * tok, tok)
 
         def expert(e, _):
-            put_z = local(zt, z_all.at[e, pl.ds(col, tok), :], lsem.at[2])
+            put_z = [local(zt.at[pl.ds(h * half, half), :], z_all.at[e, pl.ds(cols[h], half), :], lsem.at[1 + h]) for h in range(2)]
 
             def before_sum():
-                put_z.start()
+                for c in put_z:
+                    c.start()
 
                 @pl.when((e == 0) & (t == 0))
                 def _():
@@ -245,8 +266,10 @@
                     get.start()
                     get.wait()
 
-            forward(col, e, e, True, gall[slot, pl.ds(e, 1), :], t, before_sum)
-            put_z.wait()
+            gate_row = jnp.concatenate([gall[top, pl.ds(e, 1), 0:half], gall[low, pl.ds(e, 1), half:tok]], axis=1)
+            forward(cols, e, e, True, gate_row, t, before_sum)
+            for c in put_z:
+                c.wait()
             return 0
 
         lax.fori_loop(0, 2, expert, 0)
@@ -261,12 +284,9 @@
             put.start()
             put.wait()
 
-        @pl.when(j == 4)
+        @pl.when(j == 3)
         def _():
             phase1(True).start()
-
-        @pl.when(j == 5)
-        def _():
             phase1(False).start()
 
         @pl.when(j == 7)
@@ -285,7 +305,7 @@
             s = pl.ds(pl.multiple_of(base + k * rows, rows), rows)
             b = 0 if to_left else 1
             remote(opp.at[s, :], opp.at[s, :], r2s.at[b, k], r2r.at[b, k], right).wait_recv()
-            gets = [local(opp.at[s, :], acc.at[0, s, :], lsem.at[0]), local(q_sum.at[1 if to_left else 2, s, :], tmp.at[0], lsem.at[1])]
+            gets = [local(opp.at[s, :], acc.at[0, s, :], lsem.at[0]), local(q_sum.at[2, s, :], tmp.at[0], lsem.at[1])]
             for c in gets:
                 c.start()
             for c in gets:
@@ -298,43 +318,54 @@
     def column(n):
         return pl.ds(pl.multiple_of(n * cw, cw), cw)
 
-    def fetch(kind, n, b):
-        src = x_all.at[:, column(n)] if kind == 0 else z_all.at[kind - 1, :, column(n)]
-        return local(src, xc.at[b], xcs.at[b])
-
-    fetch(0, 0, 0).start()
+    deep = 4 * tok
+
+    def fetch(n, b):
+        whole = [local(x_all.at[:, column(n)], xc.at[b], xcs.at[b])]
+        for e, buf in ((0, w1v), (1, w3v)):
+            for h in range(2):
+                whole.append(local(z_all.at[e, pl.ds(h * deep, deep), column(n)], buf.at[b, pl.ds(0, deep), pl.ds(h * cw, cw)], zcs.at[e, h, b]))
+        return whole
+
+    def stage(e, kind, h):
+        if kind < 2:
+            return acc.at[1, pl.ds(0, cw), pl.ds((2 * e + kind) * ff, ff)]
+        return acc.at[1, pl.ds(cw, ff // 2), pl.ds((2 * e + h) * cw, cw)]
+
+    def results(n):
+        puts = []
+        for e in range(2):
+            puts.append(local(stage(e, 0, 0), dw1.at[e, column(n), :], o1s.at[e, 0]))
+            puts.append(local(stage(e, 1, 0), dw3.at[e, column(n), :], o1s.at[e, 1]))
+            for h in range(2):
+                puts.append(local(stage(e, 2, h), dw2.at[e, pl.ds(h * (ff // 2), ff // 2), column(n)], o2s.at[e, h]))
+        return puts
+
+    for c in fetch(0, 0):
+        c.start()
 
     def weight_grads(n, _):
-        b0 = lax.rem(3 * n, 2)
-        b1 = 1 - b0
-        fetch(1, n, b1).start()
-        fetch(0, n, b0).wait()
-        for e in range(2):
-            for h, dst in ((0, dw1), (1, dw3)):
-                put = local(o1(1, h), dst.at[e, column(n), :], o1s.at[h])
-                if e == 0:
-                    @pl.when(n > 0)
-                    def _():
-                        put.wait()
-                else:
-                    put.wait()
-                o1(1, h)[...] = jnp.transpose(dot(act[e, 1 + h], xc[b0], NN))
-                put.start()
-        fetch(2, n, b0).start()
-        for e in range(2):
-            b = b1 if e == 0 else b0
-            put = local(o2(1, e), dw2.at[e, :, column(n)], o2s.at[e])
-            fetch(1 + e, n, b).wait()
-            if e == 1:
-                @pl.when(n < chunks - 1)
-                def _():
-                    fetch(0, n + 1, b1).start()
-
-            @pl.when(n > 0)
-            def _():
-                put.wait()
-            o2(1, e)[...] = dot(act[e, 0], xc[b], NN)
-            put.start()
+        b = lax.rem(n, 2)
+        for c in fetch(n, b):
+            c.wait()
+
+        @pl.when(n > 0)
+        def _():
+            for c in results(n - 1):
+                c.wait()
+
+        @pl.when(n < chunks - 1)
+        def _():
+            for c in fetch(n + 1, 1 - b):
+                c.start()
+        for e, buf in ((0, w1v), (1, w3v)):
+            for kind in range(2):
+                stage(e, kind, 0)[...] = jnp.transpose(dot(act[e, 1 + kind], xc[b], NN))
+            for h in range(2):
+                f = slice(h * (ff // 2), (h + 1) * (ff // 2))
+                stage(e, 2, h)[...] = dot(act[e, 0, f, 0:deep], buf[b, 0:deep, 0:cw], NN) + dot(act[e, 0, f, deep:2 * deep], buf[b, 0:deep, cw:2 * cw], NN)
+        for c in results(n):
+            c.start()
 
         @pl.when(n >= chunks - 4)
         def _():
@@ -342,11 +373,9 @@
         return 0
 
     lax.fori_loop(0, chunks, weight_grads, 0)
-
-    for h, dst in ((0, dw1), (1, dw3)):
-        local(o1(1, h), dst.at[1, column(0), :], o1s.at[h]).wait()
-    for e in range(2):
-        local(o2(1, e), dw2.at[e, :, column(0)], o2s.at[e]).wait()
+    for c in results(chunks - 1):
+        c.wait()
+
     get = local(q_sum.at[0], acc.at[1], lsem.at[2])
     get.start()
     phase1(True).wait_recv()
@@ -397,8 +426,9 @@
         c.wait()
     for c in gates:
         c.wait_send()
-    for k in range(14):
-        message(k).wait_send()
+    for k in range(13):
+        for c in message(k):
+            c.wait_send()
     for to_left in (True, False):
         phase1(to_left).wait_send()
         for k in range(4):
@@ -423,8 +453,8 @@
         V((tok, dim), BF16), V((tok, dim), BF16), V((tok, dim), BF16), V((tok, ff), BF16), V((tok, ff), BF16),
         V((2, tok, dim), F32), V((2, 8 * tok, cw), BF16), V((2, tok // 8, dim), F32),
         V((8, 8, tok), F32),
-        D((3, 2)), D((8,)), D((8,)), D((14,)), D((14,)), D((4,)), D((4,)), D((2,)), D((2,)),
-        D((2, 4)), D((2, 4)), D((2, 4)), D((2, 4)), D((4,)), D((2,)), D((2,)), D((2,)), D((2, 4)),
+        D((3, 2)), D((8,)), D((8,)), D((13, 2)), D((13, 2)), D((4,)), D((4,)), D((2,)), D((2,)),
+        D((2, 4)), D((2, 4)), D((2, 4)), D((2, 4)), D((4,)), D((2,)), D((2, 2, 2)), D((2, 2)), D((2, 2)), D((2, 4)),
     ]
     any_spec = pl.BlockSpec(memory_space=pl.ANY)
     return pl.pallas_call(

time: 396 us -> 324 us (0.82)
  Pallas kernels: 360 us -> 288 us
    pallas_call x1, Pallas kernels: 360 us -> 288 us  [moe_call(): pl.pallas_call(functools.partial(moe_kernel, tok, dim, ff, cw), out_shape...]
where the time goes in v3:
time: 324 us; the launch traced here: 323 us
  Pallas kernels  288 us (89%)
  local copies, waits for them, and re-layouts  33 us (10%)
    pallas_call x1, Pallas kernels, moe_call(): pl.pallas_call(functools.partial(moe_kernel, tok, dim, ff, cw), out_shape...  288 us
    unnamed x19, local copies, waits for them, and re-layouts  30.2 us

profile of v3, /device:TPU:81, one launch (start us, length us, event | category | flops | bytes accessed | tf_op | source)
XLA Modules:
  0.0 323.1 jit_solution(2221441085498419538)
XLA Ops:
  0.6 1.2 compare_reduce_fusion.9
  1.9 1.2 fusion
  3.0 1.0 fusion.1
  4.1 0.3 and_select_fusion.9
  4.4 0.7 pad.4.gt
  5.0 287.9 %moe_backward.1 = (bf16[512,2048]{1,0:T(8,128)(2,1)}, f32[2,2048,512]{2,1,0:T(8,128)}, f32[2,2048,512]{2,1,0:T(8,128)}, f32[2,512,2048]{2,1,0:T(8,128)}, f32[204...) custom-call(bf16[512,2048]{1,0:T(8,128)(2,1)} %x_loc.1, ...), custom_call_target="tpu_custom_call" | custom-call | tf_op jit(solution)/shard_map/moe_backward/pallas_call | solution.py:460
  292.9 0.0 slice-start
  292.9 3.3 %copy.25 = bf16[512,2048]{1,0:T(8,128)(2,1)} copy(bf16[512,2048]{1,0:T(8,128)(2,1)} %get-tuple-element.58) | data formatting | bytes 4194304
  296.3 0.0 copy-start
  296.3 0.0 slice-start.1
  296.3 8.8 %copy.26 = f32[2,2048,512]{2,1,0:T(8,128)} copy(f32[2,2048,512]{2,1,0:T(8,128)} %get-tuple-element.59) | data formatting | bytes 16777216
  305.1 0.0 copy-done
  305.1 3.4 %copy.27 = f32[2,2048,512]{2,1,0:T(8,128)} copy(f32[2,2048,512]{2,1,0:T(8,128)S(1)} %copy-done) | data formatting | bytes 16777216
  308.5 0.0 slice-done
  308.5 0.0 slice-done.1
  308.5 0.0 copy-start.3
  308.5 4.3 %copy.28 = f32[2,512,2048]{2,1,0:T(8,128)} copy(f32[2,512,2048]{2,1,0:T(8,128)S(1)} %bitcast.27) | data formatting | bytes 16777216
  312.8 1.0 copy-done.3
  313.7 0.0 copy-start.2
  313.7 2.1 copy.29
  315.8 1.6 copy-done.2
  317.4 0.0 copy-start.1
  317.4 2.1 copy.30
  319.5 1.6 copy-done.1
  321.1 2.0 copy.31
  (2 shorter events, 0.0 us)
Async XLA Ops:
  292.9 15.6 %slice-start = ((s8[8388608]{0:T(1024)(128)(4,1)}), s8[4194304]{0:T(1024)(128)(4,1)S(1)}, s32[]{:S(2)}) async-start(s8[8388608]{0:T(1024)(128)(4,1)} %bitcast.26), calls=%async_computation | async-start | bytes 8388608
  296.3 8.8 %copy-start = (f32[2,2048,512]{2,1,0:T(8,128)S(1)}, f32[2,2048,512]{2,1,0:T(8,128)}, u32[]{:S(2)}) copy-start(f32[2,2048,512]{2,1,0:T(8,128)} %get-tuple-element.60) | copy-start | bytes 25165828
  296.3 12.2 %slice-start.1 = ((s8[8388608]{0:T(1024)(128)(4,1)}), s8[4194304]{0:T(1024)(128)(4,1)S(1)}, s32[]{:S(2)}) async-start(s8[8388608]{0:T(1024)(128)(4,1)} %bitcast.26), calls=%async_computation.1 | async-start | bytes 8388608
  308.5 5.2 %copy-start.3 = (f32[2048,512]{1,0:T(8,128)S(1)}, f32[2048,512]{1,0:T(8,128)}, u32[]{:S(2)}) copy-start(f32[2048,512]{1,0:T(8,128)} %get-tuple-element.18) | copy-start | bytes 12582916
  313.7 3.7 %copy-start.2 = (f32[2048,512]{1,0:T(8,128)S(1)}, f32[2048,512]{1,0:T(8,128)}, u32[]{:S(2)}) copy-start(f32[2048,512]{1,0:T(8,128)} %get-tuple-element.19) | copy-start | bytes 12582916
  317.4 3.7 %copy-start.1 = (f32[512,2048]{1,0:T(8,128)S(1)}, f32[512,2048]{1,0:T(8,128)}, u32[]{:S(2)}) copy-start(f32[512,2048]{1,0:T(8,128)} %get-tuple-element.20) | copy-start | bytes 12582916

commit v4 on v3

--- a/solution.py
+++ b/solution.py
@@ -8,6 +8,7 @@
 from jax.sharding import PartitionSpec as P
 
 CW = 256
+SENT = 2
 F32, BF16 = jnp.float32, jnp.bfloat16
 MESH = pl.DeviceIdType.MESH
 NN = (((1,), (0,)), ((), ()))
@@ -19,9 +20,9 @@
 
 
 def moe_kernel(tok, dim, ff, cw, x_loc, dy_loc, gt, w1, w3, w2, s1, s3, s2,
-               gx, dw1, dw3, dw2, sw1, sw3, sw2, x_all, dy_all, z_all, pp, q_sum, rsh, from_l, from_r, opp,
+               dw1, dw3, dw2, sw1, sw3, sw2, x_all, dy_all, z_all, pp, q_sum, rsh, from_l, from_r, late_a, late_b, opp,
                w1v, w3v, w2v, act, xt, dyt, zt, dat, dbt, acc, xc, tmp, gall,
-               wsem, gsend, grecv, ssem, rsem, psend, precv, r1s, r1r, r2s, r2r, r3s, r3r, lsem, xcs, zcs, o1s, o2s, gxs):
+               wsem, gsend, grecv, ssem, rsem, psend, precv, r1s, r1r, r2s, r2r, r3s, r3r, lsem, xcs, zcs, o1s, o2s, cs, ms):
     me = lax.axis_index("ep")
     core = lax.rem(me, 2)
     xpos = me // 2
@@ -299,19 +300,39 @@
     lax.fori_loop(0, 8, tile, 0)
     partial(3).wait_send()
 
+    def kept_sum(k, to_left):
+        s = pl.ds(pl.multiple_of((half if to_left else 0) + k * rows, rows), rows)
+        return local(acc.at[0, s, :], (late_b if to_left else late_a).at[pl.ds(pl.multiple_of((k - SENT) * rows, rows), rows), :], cs.at[1 if to_left else 0, k])
+
+    def operands(k):
+        gets = []
+        for b, base in ((1, 0), (0, half)):
+            s = pl.ds(pl.multiple_of(base + k * rows, rows), rows)
+            gets.append(local(opp.at[s, :], acc.at[0, s, :], ms.at[b, 0]))
+            gets.append(local(q_sum.at[2, s, :], tmp.at[b], ms.at[b, 1]))
+        return gets
+
+    def begin_combine(k):
+        for b, base in ((1, 0), (0, half)):
+            s = pl.ds(pl.multiple_of(base + k * rows, rows), rows)
+            remote(opp.at[s, :], opp.at[s, :], r2s.at[b, k], r2r.at[b, k], right).wait_recv()
+        for c in operands(k):
+            c.start()
+
     def combine(k):
+        for c in operands(k):
+            c.wait()
         for to_left in (False, True):
-            base = half if to_left else 0
-            s = pl.ds(pl.multiple_of(base + k * rows, rows), rows)
-            b = 0 if to_left else 1
-            remote(opp.at[s, :], opp.at[s, :], r2s.at[b, k], r2r.at[b, k], right).wait_recv()
-            gets = [local(opp.at[s, :], acc.at[0, s, :], lsem.at[0]), local(q_sum.at[2, s, :], tmp.at[0], lsem.at[1])]
-            for c in gets:
-                c.start()
-            for c in gets:
-                c.wait()
-            acc[0, s, :] += tmp[0]
-            phase3(k, to_left).start()
+            s = pl.ds(pl.multiple_of((half if to_left else 0) + k * rows, rows), rows)
+            acc[0, s, :] += tmp[0 if to_left else 1]
+
+            @pl.when(k < SENT)
+            def _():
+                phase3(k, to_left).start()
+
+            @pl.when(k >= SENT)
+            def _():
+                kept_sum(k, to_left).start()
 
     chunks = dim // cw
 
@@ -358,6 +379,10 @@
         def _():
             for c in fetch(n + 1, 1 - b):
                 c.start()
+
+        @pl.when(n >= chunks - 4)
+        def _():
+            begin_combine(n - (chunks - 4))
         for e, buf in ((0, w1v), (1, w3v)):
             for kind in range(2):
                 stage(e, kind, 0)[...] = jnp.transpose(dot(act[e, 1 + kind], xc[b], NN))
@@ -376,54 +401,13 @@
     for c in results(chunks - 1):
         c.wait()
 
-    get = local(q_sum.at[0], acc.at[1], lsem.at[2])
-    get.start()
     phase1(True).wait_recv()
     phase1(False).wait_recv()
-    get.wait()
-
-    def own_rows(k, _):
-        s = pl.ds(pl.multiple_of(k * rows, rows), rows)
-        first = local(rsh.at[s, :], tmp.at[0], lsem.at[0])
-        first.start()
-
-        @pl.when(k < 4)
-        def _():
-            local(from_r.at[s, :], tmp.at[1], lsem.at[1]).start()
-
-        @pl.when(k >= 4)
-        def _():
-            local(from_l.at[s, :], tmp.at[1], lsem.at[1]).start()
-        first.wait()
-        local(from_l.at[s, :], tmp.at[1], lsem.at[1]).wait()
-        acc[1, s, :] += tmp[0] + tmp[1]
-        return 0
-
-    lax.fori_loop(0, 8, own_rows, 0)
-
-    def last(k):
-        sa, sb = pl.ds(k * rows, rows), pl.ds(half + k * rows, rows)
-        phase3(k, False).wait_recv()
-        ga = local(from_l.at[sa, :], tmp.at[0], lsem.at[0])
-        ga.start()
-        phase3(k, True).wait_recv()
-        gb = local(from_r.at[sb, :], tmp.at[1], lsem.at[1])
-        gb.start()
-        ga.wait()
-        xt[sa, :] = (acc[1, sa, :] + tmp[0]).astype(BF16)
-        pa = local(xt.at[sa, :], gx.at[sa, :], gxs.at[0, k])
-        pa.start()
-        gb.wait()
-        xt[sb, :] = (acc[1, sb, :] + tmp[1]).astype(BF16)
-        pb = local(xt.at[sb, :], gx.at[sb, :], gxs.at[1, k])
-        pb.start()
-        return [pa, pb]
-
-    puts = []
-    for k in range(4):
-        puts += last(k)
-    for c in puts:
-        c.wait()
+    for to_left in (True, False):
+        for k in range(SENT):
+            phase3(k, to_left).wait_recv()
+        for k in range(SENT, 4):
+            kept_sum(k, to_left).wait()
     for c in gates:
         c.wait_send()
     for k in range(13):
@@ -433,6 +417,7 @@
         phase1(to_left).wait_send()
         for k in range(4):
             phase2(k, to_left).wait_send()
+        for k in range(SENT):
             phase3(k, to_left).wait_send()
 
 
@@ -442,10 +427,11 @@
     cw = CW
     sds = jax.ShapeDtypeStruct
     outs = [
-        sds((tok, dim), BF16), sds((2, dim, ff), F32), sds((2, dim, ff), F32), sds((2, ff, dim), F32),
+        sds((2, dim, ff), F32), sds((2, dim, ff), F32), sds((2, ff, dim), F32),
         sds((dim, ff), F32), sds((dim, ff), F32), sds((ff, dim), F32),
         sds((8 * tok, dim), BF16), sds((8 * tok, dim), BF16), sds((2, 8 * tok, dim), BF16),
-        sds((4, tok, dim), F32), sds((4, tok, dim), F32), sds((tok, dim), F32), sds((tok, dim), F32), sds((tok, dim), F32), sds((tok, dim), F32),
+        sds((4, tok, dim), F32), sds((4, tok, dim), F32), sds((tok, dim), F32), sds((tok, dim), F32), sds((tok, dim), F32),
+        sds(((4 - SENT) * (tok // 8), dim), F32), sds(((4 - SENT) * (tok // 8), dim), F32), sds((tok, dim), F32),
     ]
     V, D = pltpu.VMEM, pltpu.SemaphoreType.DMA
     scratch = [
@@ -454,7 +440,7 @@
         V((2, tok, dim), F32), V((2, 8 * tok, cw), BF16), V((2, tok // 8, dim), F32),
         V((8, 8, tok), F32),
         D((3, 2)), D((8,)), D((8,)), D((13, 2)), D((13, 2)), D((4,)), D((4,)), D((2,)), D((2,)),
-        D((2, 4)), D((2, 4)), D((2, 4)), D((2, 4)), D((4,)), D((2,)), D((2, 2, 2)), D((2, 2)), D((2, 2)), D((2, 4)),
+        D((2, 4)), D((2, 4)), D((2, 4)), D((2, 4)), D((4,)), D((2,)), D((2, 2, 2)), D((2, 2)), D((2, 2)), D((2, 4)), D((2, 2)),
     ]
     any_spec = pl.BlockSpec(memory_space=pl.ANY)
     return pl.pallas_call(
@@ -465,7 +451,77 @@
         scratch_shapes=scratch,
         compiler_params=pltpu.CompilerParams(collective_id=0, has_side_effects=True, vmem_limit_bytes=67043328),
         name="moe_backward",
-    )(x, dy, gt, w1, w3, w2, s1, s3, s2)[:7]
+    )(x, dy, gt, w1, w3, w2, s1, s3, s2)
+
+
+def put_kernel(q, rsh, from_l, from_r, *refs):
+    count = (len(refs) - 1) // 2
+    for src, dst in zip(refs[:count], refs[count + 1:]):
+        dst[...] = src[...]
+    base = refs[count]
+    step, steps = pl.program_id(0), pl.num_programs(0)
+    both = lax.rem(step, steps // 2) < SENT * steps // 8
+    own = q[0] + rsh[...]
+
+    @pl.when(both)
+    def _():
+        base[...] = own + (from_l[...] + from_r[...])
+
+    @pl.when(jnp.logical_not(both) & (step < steps // 2))
+    def _():
+        base[...] = own + from_r[...]
+
+    @pl.when(jnp.logical_not(both) & (step >= steps // 2))
+    def _():
+        base[...] = own + from_l[...]
+
+
+def put_out(q_sum, rsh, from_l, from_r, *arrays):
+    steps = 8
+    tok, dim = rsh.shape
+
+    def spec(a):
+        shape = a.shape[:-2] + (a.shape[-2] // steps, a.shape[-1])
+        lead = (0,) * (a.ndim - 2)
+        return pl.BlockSpec(shape, lambda i: lead + (i, 0))
+
+    size = sum(a.size * a.dtype.itemsize for a in arrays)
+    specs = [spec(a) for a in arrays]
+    row = pl.BlockSpec((tok // steps, dim), lambda i: (i, 0))
+    return pl.pallas_call(
+        put_kernel, grid=(steps,),
+        in_specs=[pl.BlockSpec((1, tok // steps, dim), lambda i: (0, i, 0)), row, row, row] + specs,
+        out_specs=[row] + specs,
+        out_shape=[jax.ShapeDtypeStruct((tok, dim), F32)] + [jax.ShapeDtypeStruct(a.shape, a.dtype) for a in arrays],
+        compiler_params=pltpu.CompilerParams(vmem_limit_bytes=67043328),
+        cost_estimate=pl.CostEstimate(flops=size * 1000, bytes_accessed=2 * size, transcendentals=0),
+        name="put_out",
+    )(q_sum, rsh, from_l, from_r, *arrays)
+
+
+def last_kernel(base, late_l, late_r, out):
+    done = SENT * base.shape[0] // 4
+    out[:done] = base[:done].astype(BF16)
+
+    @pl.when(pl.program_id(0) == 0)
+    def _():
+        out[done:] = (base[done:] + late_l[...]).astype(BF16)
+
+    @pl.when(pl.program_id(0) == 1)
+    def _():
+        out[done:] = (base[done:] + late_r[...]).astype(BF16)
+
+
+def last_sum(base, late_l, late_r):
+    tok, dim = base.shape
+    row = pl.BlockSpec((tok // 2, dim), lambda i: (i, 0))
+    late = pl.BlockSpec(late_l.shape, lambda i: (0, 0))
+    return pl.pallas_call(
+        last_kernel, grid=(2,), in_specs=[row, late, late], out_specs=row,
+        out_shape=jax.ShapeDtypeStruct((tok, dim), BF16),
+        compiler_params=pltpu.CompilerParams(vmem_limit_bytes=67043328),
+        name="last_sum",
+    )(base, late_l, late_r)
 
 
 def solution(mesh):
@@ -484,7 +540,12 @@
         for j in range(top_k):
             table = jnp.where((ids[j:j + 1] == experts) & (pos[j:j + 1] >= 0), gates[j:j + 1], table)
         table = jnp.pad(table.reshape(group, -1, tok_count), ((0, 0), (0, 8 - num_experts // group), (0, 0)))
-        gx, dw1, dw3, dw2, sw1, sw3, sw2 = moe_call(x_tokens, dy_tokens, table, w_gate, w_up, w_down, shared_gate, shared_up, shared_down)
+        dw1, dw3, dw2, sw1, sw3, sw2, _, _, _, _, q_sum, rsh, from_l, from_r, late_a, late_b, _ = moe_call(x_tokens, dy_tokens, table, w_gate, w_up, w_down, shared_gate, shared_up, shared_down)
+        ring = [2 * ((i // 2 + 1) % (group // 2)) + i % 2 for i in range(group)]
+        late_l = lax.ppermute(late_a, 'ep', [(i, r) for i, r in enumerate(ring)])
+        late_r = lax.ppermute(late_b, 'ep', [(r, i) for i, r in enumerate(ring)])
+        base, dw1, dw3, dw2, sw1, sw3, sw2 = put_out(q_sum, rsh, from_l, from_r, dw1, dw3, dw2, sw1, sw3, sw2)
+        gx = last_sum(base, late_l, late_r)
         return gx, dw1, dw3, dw2, sw1[None], sw3[None], sw2[None]
 
     return jax.shard_map(local_backward, mesh=mesh, in_specs=(token_spec, token_spec, token_spec, token_spec, token_spec, expert_spec, expert_spec, expert_spec, whole_spec, whole_spec, whole_spec), out_specs=(token_spec, grad_spec, grad_spec, grad_spec, grad_spec, grad_spec, grad_spec), check_vma=False)

time: 324 us -> 307 us (0.948)
  local copies, waits for them, and re-layouts: 33 us -> 2.86 us
  Pallas kernels: 288 us -> 299 us
    pallas_call x0 -> x2, Pallas kernels: none -> 35.5 us  [the longest x1 31.5 us: put_out(): pl.pallas_call(put_kernel, grid=(steps,), in_specs=[pl.BlockSpec((1, tok...]
    unnamed x19 -> x0, local copies, waits for them, and re-layouts: 30.2 us -> none
    pallas_call x1, Pallas kernels: 288 us -> 264 us  [moe_call(): pl.pallas_call(functools.partial(moe_kernel, tok, dim, ff, cw), out_shape...]
  transfers between devices with their start and end apart: 0 -> 2, of which waited for: 0 -> 0; matrix products, arithmetic and copies ran while one was open for 0% -> 0% of each run, Pallas kernels for 0% -> 10%
where the time goes in v4:
time: 307 us
  Pallas kernels  299 us (97%)
    pallas_call x1, Pallas kernels, moe_call(): pl.pallas_call(functools.partial(moe_kernel, tok, dim, ff, cw), out_shape...  264 us
    pallas_call x1, Pallas kernels, put_out(): pl.pallas_call(put_kernel, grid=(steps,), in_specs=[pl.BlockSpec((1, tok...  31.5 us
  transfers between devices with their start and end apart: 2, of which 0 were waited for; matrix products, arithmetic and copies ran while one was open for 0% of the time, Pallas kernels for 10%

profile of v4, /device:TPU:81, one launch (start us, length us, event | category | flops | bytes accessed | tf_op | source)
XLA Modules:
  0.0 306.9 jit_solution(12023197721523119716)
XLA Ops:
  0.6 1.2 compare_reduce_fusion.9
  1.9 1.2 fusion
  3.0 1.0 fusion.1
  4.1 0.3 and_select_fusion.9
  4.4 0.7 pad.4.gt
  5.0 263.5 %moe_backward.1 = (f32[2,2048,512]{2,1,0:T(8,128)}, f32[2,2048,512]{2,1,0:T(8,128)}, f32[2,512,2048]{2,1,0:T(8,128)}, f32[2048,512]{1,0:T(8,128)}, f32[2048,512]...) custom-call(bf16[512,2048]{1,0:T(8,128)(2,1)} %x_loc.1, ...), custom_call_target="tpu_custom_call" | custom-call | tf_op jit(solution)/shard_map/moe_backward/pallas_call | solution.py:446
  268.5 0.1 collective-permute-start
  268.7 2.6 collective-permute-start.1
  271.3 31.5 %put_out.1 = (f32[512,2048]{1,0:T(8,128)}, f32[2,2048,512]{2,1,0:T(8,128)}, f32[2,2048,512]{2,1,0:T(8,128)}, f32[2,512,2048]{2,1,0:T(8,128)}, f32[2048,512]{1,0:...) custom-call(f32[4,512,2048]{2,1,0:T(8,128)} %get-tuple-element.26.q, f32[512,2048]{1,0:T(8,128)} %get-tuple-element.27.rsh, ...), custom_call_target="tpu_custom_call" | custom-call | flops 37748736000 | bytes 75497472 | tf_op jit(solution)/shard_map/put_out/pallas_call | solution.py:491
  302.8 0.0 collective-permute-done.late_l
  302.9 0.0 collective-permute-done.1.late_r
  302.9 4.0 %last_sum.1 = bf16[512,2048]{1,0:T(8,128)(2,1)} custom-call(f32[512,2048]{1,0:T(8,128)} %get-tuple-element.36.base, f32[128,2048]{1,0:T(8,128)} %collective-permute-done.late_l, f32[128,2048]{1,0:T(8,128)} %collective-permute-done.1.late_r), custom_call_target="tpu_custom_call" | custom-call | tf_op jit(solution)/shard_map/last_sum/pallas_call | solution.py:519
  (1 shorter events, 0.0 us)
Async XLA Ops:
  268.5 34.3 %collective-permute-start = (f32[128,2048]{1,0:T(8,128)}, f32[128,2048]{1,0:T(8,128)}, u32[]{:S(2)}, u32[]{:S(2)}) collective-permute-start(f32[128,2048]{1,0:T(8,128)} %get-tuple-element.37), channel_id=1, source_target_pairs={{0,2},{1,3},{2,4},{3,5},{4,6},{5,7},{6,0},{7,1},{8,10},{9,11},{10,... | collective-permute-start | bytes 3145736 | tf_op jit(solution)/shard_map/ppermute | solution.py:545
  268.7 34.2 %collective-permute-start.1 = (f32[128,2048]{1,0:T(8,128)}, f32[128,2048]{1,0:T(8,128)}, u32[]{:S(2)}, u32[]{:S(2)}) collective-permute-start(f32[128,2048]{1,0:T(8,128)} %get-tuple-element.38), channel_id=1, source_target_pairs={{2,0},{3,1},{4,2},{5,3},{6,4},{7,5},{0,6},{1,7},{10,8},{11,9},{12,... | collective-permute-start | bytes 3145736 | tf_op jit(solution)/shard_map/ppermute | solution.py:546
